TPU v7x, 256 devices: a 4x2x16 block of a 4x16x16 slice. The times are simulated.
256 devices in a mesh: grp: 2 (over y), tm: 128 (over x, z, core).
Axes of the slice: x: 4, y: 2, z: 16, core: 2. Of those that a mesh axis runs over, the one named last changes fastest.
The devices are a block of a 4x16x16 slice.
Arguments:
- traces: float32 [2048, 16384], P('grp', 'tm'), parts along dimension 0, may hold values from -6 to 6
- templates: float32 [512, 8192], P('tm'), may hold values from -6 to 6
- moveouts: int32 [2048], P('grp'), parts along dimension 0, may hold values from 0 to 2047
- masks: int32 [512, 2048], P(None, 'grp'), parts along dimension 1, may hold values 0 or 1
Outputs:
- detection: float32 [512, 16384], P('tm', 'grp'), parts along dimension 1
There are 2 independent parts, one for each index of `grp`. A program takes and returns all parts, laid end to end along the dimension named above; an argument that names none is the same for every part. Nothing has to cross between parts.
All inputs are finite; a program needn't handle non-finite values.
Results may differ from a plain program's by a relative error of at most 0.000073.
Values sent between devices are 32-bit elements; how exact they have to be, the bound alone decides.
A program may use at most 64 MiB of HBM per device.

v0:
```python
import functools
import math

import jax
import jax.numpy as jnp
import numpy as np
from jax import lax
from jax.experimental import pallas as pl
from jax.experimental.pallas import tpu as pltpu
from jax.sharding import Mesh
from jax.sharding import PartitionSpec as P

MESH = pl.DeviceIdType.MESH
LANES = 128
GROUP = 2


def split(value):
    high = value.astype(jnp.bfloat16)
    low = (value - high.astype(jnp.float32)).astype(jnp.bfloat16)
    return high, low


def split_constant(value):
    value = np.asarray(value, np.float64).astype(np.float32)
    high = value.astype(jnp.bfloat16)
    low = (value - high.astype(np.float32)).astype(jnp.bfloat16)
    return jnp.asarray(np.stack([high, low]))


def mm(a, b):
    return jnp.dot(a, b, preferred_element_type=jnp.float32)


def dot3(left, right):
    (left_hi, left_lo), (right_hi, right_lo) = left, right
    return mm(left_hi, right_hi) + (mm(left_hi, right_lo) + mm(left_lo, right_hi))


def stack_kernel(
    cfg, x_hbm, masks_hbm, mo_ref, out_ref,
    pair, mask_int, mask_rows, rolled, shift_at, parts, partial, up, down, ready, landed,
    load_sem, pair_sem, up_send, up_recv, down_send, down_recv, last_send, last_recv,
):
    rows, ring, hops, above, below = cfg
    channels = x_hbm.shape[0]
    blocks = rows * ring
    chip_samples = 2 * LANES
    x = lax.axis_index("tm_0")
    z = lax.axis_index("tm_1")
    core = lax.axis_index("tm_2")
    here = x * ring + z

    def far(dx, dz):
        return {"tm_0": lax.rem(x + dx + rows, rows), "tm_1": lax.rem(z + dz + ring, ring)}

    def chip(step):
        other = lax.rem(here + step + blocks, blocks)
        return {"tm_0": other // ring, "tm_1": lax.rem(other, ring)}

    barrier = pltpu.get_barrier_semaphore()
    pl.semaphore_signal(barrier, inc=1, device_id={"tm_2": 1 - core}, device_id_type=MESH)
    senders = 1
    for dz in range(-above, below + 1):
        for dx in range(rows):
            if dx or dz:
                pl.semaphore_signal(barrier, inc=1, device_id=far(dx, dz), device_id_type=MESH)
                senders += 1

    mask_copy = pltpu.make_async_copy(masks_hbm, mask_int, load_sem.at[0])
    mask_copy.start()
    own_copy = pltpu.make_async_copy(x_hbm, pair.at[core], load_sem.at[1])
    own_copy.start()
    mask_copy.wait()

    tile_rows = mask_int.shape[2]
    half_tile = tile_rows // 2
    tops = lax.broadcasted_iota(jnp.int32, (tile_rows, channels), 0) < half_tile

    def pick(first, second):
        moved = pltpu.roll(jnp.where(core == 0, second, first), half_tile, 0)
        kept = jnp.where(core == 0, first, second)
        return jnp.where(tops == (core == 0), kept, moved)

    @pl.loop(0, ring)
    def _(e):
        owner = lax.rem(z + e, ring)
        pieces = [
            pick(mask_int[a, owner], mask_int[a + 1, owner]).astype(jnp.float32) for a in range(0, rows, 2)
        ]
        mask_rows[e] = jnp.concatenate(pieces, axis=0).astype(jnp.bfloat16)

    own_copy.wait()
    pl.semaphore_wait(barrier, senders)
    swap = pltpu.make_async_remote_copy(
        src_ref=pair.at[core],
        dst_ref=pair.at[core],
        send_sem=pair_sem.at[0],
        recv_sem=pair_sem.at[1],
        device_id={"tm_2": 1 - core},
        device_id_type=MESH,
    )
    swap.start()
    swap.wait()

    lane = lax.broadcasted_iota(jnp.int32, (LANES, LANES), 1)

    @pl.loop(0, channels // LANES)
    def _(b):
        at = pl.ds(pl.multiple_of(b * LANES, LANES), LANES)
        spread = jnp.broadcast_to(mo_ref[pl.ds(b, 1), :].astype(jnp.float32), (LANES, LANES))
        move = jnp.transpose(spread).astype(jnp.int32)
        fine = lax.rem(move, chip_samples)
        coarse = move // chip_samples
        first, second = pair[0, at, :], pair[1, at, :]
        swapped = fine >= LANES
        first, second = jnp.where(swapped, second, first), jnp.where(swapped, first, second)
        k = 1
        while k < LANES:
            taken = (fine & k) != 0
            inside = lane < LANES - k
            a, d = pltpu.roll(first, LANES - k, 1), pltpu.roll(second, LANES - k, 1)
            first, second = (
                jnp.where(taken, jnp.where(inside, a, d), first),
                jnp.where(taken, jnp.where(inside, d, a), second),
            )
            k *= 2
        rolled[at, :LANES] = first
        rolled[at, LANES:] = second
        shift_at[at, :LANES] = coarse + (lane >= chip_samples - fine).astype(jnp.int32)
        shift_at[at, LANES:] = coarse + (lane + LANES >= chip_samples - fine).astype(jnp.int32)

    def contribution(j):
        @pl.loop(0, channels // LANES)
        def _(b):
            at = pl.ds(pl.multiple_of(b * LANES, LANES), LANES)
            high, low = split(jnp.where(shift_at[at, :] == j, rolled[at, :], 0.0))
            parts[0, at, :] = high
            parts[1, at, :] = low

        weights = mask_rows[...].reshape(-1, channels)
        total = mm(weights, parts[0]) + mm(weights, parts[1])
        partial[j] = total.reshape(partial.shape[1:])

    @pl.loop(0, 2)
    def _(t):
        contribution(t * hops)

    sends = []

    def send(src, dst, send_sem, recv_sem, where):
        copy = pltpu.make_async_remote_copy(
            src_ref=src, dst_ref=dst, send_sem=send_sem, recv_sem=recv_sem, device_id=where, device_id_type=MESH
        )
        copy.start()
        sends.append(copy)

    up_groups = [(max(top - GROUP + 1, 1), top) for top in range(above_top(cfg), 0, -GROUP)]
    down_groups = [
        (low, min(low + GROUP - 1, hops - 1)) for low in range(-below, hops, GROUP)
    ]
    upward, downward = chip(1), chip(-1)

    def up_range(j, g):
        low, top = up_groups[g]
        low = max(low, j + 1)
        return (low - j, top - low + 1) if low <= top else None

    def down_range(j, g):
        low, top = down_groups[g]
        top = min(top, j - 1)
        return (low - j, top - low + 1) if low <= top else None

    def send_up(j, g):
        found = up_range(j, g)
        if found is None or j == hops:
            return
        e, count = found
        src = partial.at[0, pl.ds(e, count)] if j == 0 else up.at[j - 1, pl.ds(e, count)]
        send(src, up.at[j, pl.ds(e - 1, count)], up_send.at[j, g], up_recv.at[j, g], upward)

    def send_down(j, g):
        found = down_range(j, g)
        if found is None or j == 0:
            return
        e, count = found
        if j == hops:
            src = partial.at[hops, pl.ds(e + ring, count)]
        else:
            src = down.at[j, pl.ds(e + ring, count)]
        send(src, down.at[j - 1, pl.ds(e + 1 + ring, count)], down_send.at[j - 1, g], down_recv.at[j - 1, g], downward)

    for g in range(max(len(up_groups), len(down_groups))):
        if g < len(up_groups):
            send_up(0, g)
        if g < len(down_groups):
            send_down(hops, g)

    @pl.loop(1, hops)
    def _(j):
        contribution(j)

    per_owner = partial.shape[2] // rows

    def deliver(total, o, j, e):
        for a in range(rows):
            piece = total[a * per_owner : (a + 1) * per_owner]
            ready[o + below, a] = jnp.concatenate([piece[:, :LANES], piece[:, LANES:]], axis=0)
        block = lax.rem(here - j + blocks, blocks)
        for d in range(rows):
            owner = lax.rem(x + d, rows)
            src, dst = ready.at[o + below, owner], landed.at[block]
            if d == 0 and e == 0:
                copy = pltpu.make_async_copy(src, dst, last_recv)
                copy.start()
            else:
                send(src, dst, last_send.at[o + below, d], last_recv, far(d, e))

    def wait_for(ref, sem):
        pltpu.make_async_copy(ref, ref, sem).wait()

    for step in range(1, hops + 1):
        j, i = step, hops - step
        for g in range(max(len(up_groups), len(down_groups))):
            if g < len(up_groups):
                arrived = up_range(j - 1, g)
                if arrived is not None:
                    e, count = arrived[0] - 1, arrived[1]
                    wait_for(up.at[j - 1, pl.ds(e, count)], up_recv.at[j - 1, g])
                    for c in range(e, e + count):
                        if c > 0:
                            up[j - 1, c] = up[j - 1, c] + partial[j, c]
                    send_up(j, g)
            if g < len(down_groups):
                arrived = down_range(i + 1, g)
                if arrived is not None:
                    e, count = arrived[0] + 1, arrived[1]
                    wait_for(down.at[i, pl.ds(e + ring, count)], down_recv.at[i, g])
                    for c in range(e, e + count):
                        if c < 0:
                            down[i, c + ring] = down[i, c + ring] + partial[i, c + ring]
                    send_down(i, g)
        if j == hops:
            for o in range(above_top(cfg), hops, -1):
                deliver(up[j - 1, o - j], o, j, o - j)
            for o in range(-below, 0):
                deliver(down[0, o + ring], o, 0, o)
        ends = [j, i] if j > i else [j] if j == i else []
        for at in ends:
            total = partial[at, 0]
            if at > 0:
                total = total + up[at - 1, 0]
            if at < hops:
                total = total + down[at, ring]
            deliver(total, at, at, 0)

    wait_for(landed, last_recv)
    out_ref[...] = landed[...]
    for copy in sends:
        copy.wait_send()


def above_top(cfg):
    return cfg[2] + cfg[3]


def forward(series, first, twiddle, second):
    half = twiddle.shape[1]
    turned = []
    for s in series:
        y = dot3((first[0], first[1]), split(s))
        re, im = y[:half], y[half:]
        turned.append(
            jnp.concatenate(
                [re * twiddle[0] - im * twiddle[1], re * twiddle[1] + im * twiddle[0]], axis=1
            )
        )
    return dot3(split(jnp.concatenate(turned, axis=0)), (second[0], second[1]))


def correlate_kernel(
    scale, stack_ref, templ_ref, first_ref, first_half_ref, twiddle_ref, second_ref, third_ref, fourth_ref, out_ref
):
    count = out_ref.shape[1]
    long, short = stack_ref.shape[0] // count, templ_ref.shape[0] // count
    half = twiddle_ref.shape[1]
    templates = [templ_ref[pl.ds(i, short, stride=count), :] for i in range(count)]
    series = [stack_ref[pl.ds(i, long, stride=count), :] for i in range(count)]
    twiddle = twiddle_ref[...]
    second = second_ref[...]
    templ = forward(templates, first_half_ref[...], twiddle, second)
    spec = forward(series, first_ref[...], twiddle, second)
    sr, si, hr, hi = spec[:, :LANES], spec[:, LANES:], templ[:, :LANES], templ[:, LANES:]
    product = jnp.concatenate([sr * hr + si * hi, si * hr - sr * hi], axis=1)
    third = third_ref[...]
    back = dot3(split(product), (third[0], third[1]))
    fourth = fourth_ref[...]
    for i in range(count):
        re, im = back[i * half : (i + 1) * half, :LANES], back[i * half : (i + 1) * half, LANES:]
        turned = jnp.concatenate(
            [re * twiddle[0] + im * twiddle[1], im * twiddle[0] - re * twiddle[1]], axis=0
        )
        lags = dot3((fourth[0], fourth[1]), split(turned))
        energy = jnp.sqrt(jnp.sum(templates[i] * templates[i], keepdims=True) + 1e-06)
        out_ref[:, i, :] = lags * (1.0 / (scale * energy))


def fourier_tables(length, lag_count):
    blocks = length // LANES
    kept = blocks // 2 + 1
    half = -(-kept // 8) * 8
    f1 = np.arange(half)
    n1 = np.arange(blocks)
    n2 = np.arange(LANES)
    live = (f1 < kept)[:, None]
    angle = 2.0 * np.pi * ((f1[:, None] * n1[None, :]) % blocks) / blocks
    first = np.concatenate([np.cos(angle) * live, -np.sin(angle) * live])
    turn = 2.0 * np.pi * ((f1[:, None] * n2[None, :]) % length) / length
    twiddle = np.stack([np.cos(turn) * live, -np.sin(turn) * live]).astype(np.float32)
    inner = 2.0 * np.pi * ((n2[:, None] * n2[None, :]) % LANES) / LANES
    c, s = np.cos(inner), np.sin(inner)
    second = np.block([[c, -s], [s, c]])
    third = np.block([[c, s], [-s, c]])
    weight = np.where((f1 == 0) | (f1 == kept - 1), 1.0, 2.0) * (f1 < kept) / length
    lag_rows = lag_count // LANES
    back = angle.T[:lag_rows]
    fourth = np.concatenate([np.cos(back) * weight, -np.sin(back) * weight], axis=1)
    return (
        split_constant(first),
        split_constant(first[:, :lag_rows]),
        jnp.asarray(twiddle),
        split_constant(second),
        split_constant(third),
        split_constant(fourth),
    )


def on_device(traces, templates, moveouts, masks):
    rows, ring = lax.axis_size("tm_0"), lax.axis_size("tm_1")
    channels, samples = traces.shape
    devices = rows * ring * 2
    length = samples * devices
    count, lag_count = templates.shape
    chip_samples = 2 * samples
    hops = (length // 8) // chip_samples
    outside = ring - 1 - hops
    below = outside // 2
    above = outside - below
    cfg = (rows, ring, hops, above, below)
    chunk = (rows * count, chip_samples)
    groups_up = -(-(hops + above) // GROUP)
    groups_down = -(-(hops + below) // GROUP)
    vmem = pl.BlockSpec(memory_space=pltpu.VMEM)
    anywhere = pl.BlockSpec(memory_space=pl.ANY)
    dma = pltpu.SemaphoreType.DMA
    stacked = pl.pallas_call(
        functools.partial(stack_kernel, cfg),
        out_shape=jax.ShapeDtypeStruct((rows * ring, 2 * count, LANES), jnp.float32),
        in_specs=[anywhere, anywhere, vmem],
        out_specs=vmem,
        scratch_shapes=[
            pltpu.VMEM((2, channels, samples), jnp.float32),
            pltpu.VMEM((rows, ring, 2 * count, channels), jnp.int32),
            pltpu.VMEM((ring, rows * count, channels), jnp.bfloat16),
            pltpu.VMEM((channels, chip_samples), jnp.float32),
            pltpu.VMEM((channels, chip_samples), jnp.int32),
            pltpu.VMEM((2, channels, chip_samples), jnp.bfloat16),
            pltpu.VMEM((hops + 1, ring, *chunk), jnp.float32),
            pltpu.VMEM((hops, hops + above, *chunk), jnp.float32),
            pltpu.VMEM((hops, ring + 1, *chunk), jnp.float32),
            pltpu.VMEM((ring, rows, 2 * count, LANES), jnp.float32),
            pltpu.VMEM((rows * ring, 2 * count, LANES), jnp.float32),
            dma((2,)),
            dma((2,)),
            dma((hops, groups_up)),
            dma((hops, groups_up)),
            dma((hops, groups_down)),
            dma((hops, groups_down)),
            dma((ring, rows)),
            dma,
        ],
        compiler_params=pltpu.CompilerParams(collective_id=0, has_side_effects=True),
    )(
        traces,
        masks.reshape(rows, ring, 2 * count, channels),
        moveouts.reshape(channels // LANES, LANES),
    )
    lag_rows = lag_count // LANES
    tiles = templates.reshape(count, lag_rows, LANES).transpose(1, 0, 2).reshape(lag_rows * count, LANES)
    scale = math.sqrt(channels)
    tables = fourier_tables(length, lag_count)
    found = pl.pallas_call(
        functools.partial(correlate_kernel, scale),
        out_shape=jax.ShapeDtypeStruct((lag_rows, count, LANES), jnp.float32),
        in_specs=[vmem] * (2 + len(tables)),
        out_specs=vmem,
    )(stacked.reshape(-1, LANES), tiles, *tables)
    return found.transpose(1, 0, 2).reshape(count, lag_count)


def solution(mesh):
    finer = Mesh(mesh.devices.reshape(mesh.shape["grp"], 4, -1, 2), ("grp", "tm_0", "tm_1", "tm_2"))
    axes = ("tm_0", "tm_1", "tm_2")
    return jax.shard_map(
        on_device,
        mesh=finer,
        in_specs=(P("grp", axes), P(axes, None), P("grp"), P(None, "grp")),
        out_specs=P(axes, "grp"),
        check_vma=False,
    )
```

profile of v0, /device:TPU:40, one launch (start us, length us, event | category | flops | bytes accessed | tf_op | source)
XLA Modules:
  0.0 81.4 jit_solution(16435176477785816284)
XLA Ops:
  0.0 77.9 %shard_map.100 = f32[64,8,128]{2,1,0:T(8,128)} custom-call(f32[1024,128]{1,0:T(8,128)} %x_hbm.1, s32[4,16,8,1024]{3,2,1,0:T(8,128)} %bitcast.11, s32[8,128]{1,0:T(8,128)} %bitcast.14), custom_call_target="tpu_custom_call" | custom-call | tf_op jit(solution)/shard_map/pallas_call | solution.py:356
  77.9 3.5 %shard_map.101 = f32[64,4,128]{2,1,0:T(4,128)} custom-call(f32[512,128]{1,0:T(8,128)} %bitcast.12, f32[256,128]{1,0:T(8,128)} %bitcast.13, bf16[2,144,128]{2,1,0:T(8,128)(2,1)} %constant.12.clone.first_ref, bf16[2,144,64]{2,1,0:T(8,128)(2,1)} %constant.13.clone.first_half_ref, f32[2,72,128]{2,1,0:T(8,128)} %constant.14.clone.twiddle_ref, ...), custom_call_target="tpu_custom_call" | custom-call | tf_op jit(solution)/shard_map/pallas_call | solution.py:392
where the time goes:
time: 81.6 us; the launch traced here: 81.4 us
  Pallas kernels  81.4 us (100%)
    pallas_call x1, Pallas kernels, on_device(): pl.pallas_call(functools.partial(stack_kernel, cfg), out_shape=jax.ShapeD...  77.9 us
    pallas_call x1, Pallas kernels, on_device(): pl.pallas_call(functools.partial(correlate_kernel, scale), out_shape=jax....  3.51 us

commit v1 on v0

v1 whole, which is shorter than its diff:
```python
import functools
import math

import jax
import jax.numpy as jnp
import numpy as np
from jax import lax
from jax.experimental import pallas as pl
from jax.experimental.pallas import tpu as pltpu
from jax.sharding import Mesh
from jax.sharding import PartitionSpec as P

MESH = pl.DeviceIdType.MESH
LANES = 128
GROUP = 2
PIECES = 4


def split(value):
    high = value.astype(jnp.bfloat16)
    low = (value - high.astype(jnp.float32)).astype(jnp.bfloat16)
    return high, low


def split_constant(value):
    value = np.asarray(value, np.float64).astype(np.float32)
    high = value.astype(jnp.bfloat16)
    low = (value - high.astype(np.float32)).astype(jnp.bfloat16)
    return jnp.asarray(np.stack([high, low]))


def mm(a, b):
    return jnp.dot(a, b, preferred_element_type=jnp.float32)


def dot3(left, right):
    (left_hi, left_lo), (right_hi, right_lo) = left, right
    return mm(left_hi, right_hi) + (mm(left_hi, right_lo) + mm(left_lo, right_hi))


def forward(series, first, twiddle, second):
    half = twiddle.shape[1]
    turned = []
    for s in series:
        y = dot3((first[0], first[1]), split(s))
        re, im = y[:half], y[half:]
        turned.append(
            jnp.concatenate([re * twiddle[0] - im * twiddle[1], re * twiddle[1] + im * twiddle[0]], axis=1)
        )
    return dot3(split(jnp.concatenate(turned, axis=0)), (second[0], second[1]))


def matched_kernel(
    cfg, scale,
    x_hbm, masks_hbm, mo_hbm, templ_hbm, first_hbm, first_half_hbm, twiddle_hbm, second_hbm, third_hbm, fourth_hbm,
    out_ref,
    raw, mo_ref, pair, mask_int, mask_rows, halves, shift_at, parts, partial, up, down, ready, landed,
    templ_ref, first_ref, first_half_ref, twiddle_ref, second_ref, third_ref, fourth_ref, templ_spec, gain,
    load_sem, pair_send, pair_recv, up_send, up_recv, down_send, down_recv, last_send, last_recv,
):
    rows, ring, hops, above, below, shared = cfg
    channels = x_hbm.shape[0]
    blocks = rows * ring
    x = lax.axis_index("tm_0")
    z = lax.axis_index("tm_1")
    core = lax.axis_index("tm_2")
    here = x * ring + z
    partner = {"tm_2": 1 - core}

    def chip(step):
        other = lax.rem(here + step + blocks, blocks)
        return {"tm_0": other // ring, "tm_1": lax.rem(other, ring)}

    loads = []

    def load(src, dst):
        copy = pltpu.make_async_copy(src, dst, load_sem.at[len(loads)])
        copy.start()
        loads.append(copy)
        return copy

    per_piece = channels // PIECES
    mo_copy = load(mo_hbm, mo_ref)
    x_copies = [load(x_hbm.at[pl.ds(p * per_piece, per_piece)], raw.at[pl.ds(p * per_piece, per_piece)]) for p in range(PIECES)]

    barrier = pltpu.get_barrier_semaphore()
    pl.semaphore_signal(barrier, inc=1, device_id=partner, device_id_type=MESH)
    senders = 1
    reach = max(above, below) + shared
    for dz in range(-reach, reach + 1):
        for dx in range(rows):
            if dx or dz:
                where = {"tm_0": lax.rem(x + dx, rows), "tm_1": lax.rem(z + dz + ring, ring)}
                pl.semaphore_signal(barrier, inc=1, device_id=where, device_id_type=MESH)
                senders += 1

    mask_copy = load(masks_hbm, mask_int)
    templ_copy = load(templ_hbm, templ_ref)
    table_copies = [
        load(first_half_hbm, first_half_ref),
        load(twiddle_hbm, twiddle_ref),
        load(second_hbm, second_ref),
        load(first_hbm, first_ref),
        load(third_hbm, third_ref),
        load(fourth_hbm, fourth_ref),
    ]

    lane = lax.broadcasted_iota(jnp.int32, (LANES, LANES), 1)
    mo_copy.wait()
    swaps = []
    for p in range(PIECES):
        x_copies[p].wait()

        @pl.loop(p * per_piece // LANES, (p + 1) * per_piece // LANES)
        def _(b):
            at = pl.ds(pl.multiple_of(b * LANES, LANES), LANES)
            spread = jnp.broadcast_to(mo_ref[pl.ds(b, 1), :].astype(jnp.float32), (LANES, LANES))
            move = jnp.transpose(spread).astype(jnp.int32)
            index = lane + (move & (LANES - 1))
            value = jnp.take_along_axis(raw[at, :], index & (LANES - 1), axis=1)
            pair[core, at, :] = value
            passed = (index >= LANES).astype(jnp.int32)
            shift_at[at, :] = ((move >> (LANES.bit_length() - 1)) + passed).astype(jnp.float32).astype(jnp.bfloat16)
            high, low = split(value)
            halves[0, core, at, :] = high
            halves[1, core, at, :] = low

        if p == 0:
            pl.semaphore_wait(barrier, senders)
        half = pair.at[core, pl.ds(p * per_piece, per_piece)]
        swap = pltpu.make_async_remote_copy(
            src_ref=half, dst_ref=half, send_sem=pair_send.at[p], recv_sem=pair_recv.at[p],
            device_id=partner, device_id_type=MESH,
        )
        swap.start()
        swaps.append(swap)

    mask_copy.wait()
    tile_rows = mask_int.shape[2]
    half_tile = tile_rows // 2
    tops = lax.broadcasted_iota(jnp.int32, (tile_rows, channels), 0) < half_tile

    def pick(first, second):
        moved = pltpu.roll(jnp.where(core == 0, second, first), half_tile, 0)
        kept = jnp.where(core == 0, first, second)
        return jnp.where(tops == (core == 0), kept, moved)

    @pl.loop(0, ring)
    def _(e):
        owner = lax.rem(z + e, ring)
        pieces = [
            pick(mask_int[a, owner], mask_int[a + 1, owner]).astype(jnp.float32) for a in range(0, rows, 2)
        ]
        mask_rows[e] = jnp.concatenate(pieces, axis=0).astype(jnp.bfloat16)

    for p in range(PIECES):
        swaps[p].wait_recv()

        @pl.loop(p * per_piece // LANES, (p + 1) * per_piece // LANES)
        def _(b):
            at = pl.ds(pl.multiple_of(b * LANES, LANES), LANES)
            high, low = split(pair[1 - core, at, :])
            halves[0, 1 - core, at, :] = high
            halves[1, 1 - core, at, :] = low

    zero = jnp.zeros((LANES, LANES), jnp.bfloat16)

    def contribution(j):
        twice = jnp.broadcast_to((2 * j).astype(jnp.float32), (LANES, LANES))
        before, same, after = ((twice + d).astype(jnp.bfloat16) for d in (-1, 0, 1))

        @pl.loop(0, channels // LANES)
        def _(b):
            at = pl.ds(pl.multiple_of(b * LANES, LANES), LANES)
            shift = shift_at[at, :]
            is_before, is_same, is_after = shift == before, shift == same, shift == after
            for t in range(2):
                first, second = halves[t, 0, at, :], halves[t, 1, at, :]
                parts[t, at, :LANES] = jnp.where(is_same, first, jnp.where(is_after, second, zero))
                parts[t, at, LANES:] = jnp.where(is_before, first, jnp.where(is_same, second, zero))

        weights = mask_rows[...].reshape(-1, channels)
        total = mm(weights, parts[0]) + mm(weights, parts[1])
        partial[j] = total.reshape(partial.shape[1:])

    def contributions(s):
        if s == hops - s:
            contribution(jnp.int32(s))
        else:
            @pl.loop(0, 2)
            def _(t):
                contribution(s + t * (hops - 2 * s))

    contributions(0)

    sends = []

    def send(src, dst, send_sem, recv_sem, where):
        copy = pltpu.make_async_remote_copy(
            src_ref=src, dst_ref=dst, send_sem=send_sem, recv_sem=recv_sem, device_id=where, device_id_type=MESH
        )
        copy.start()
        sends.append(copy)

    chunk_rows = partial.shape[2]
    part = chunk_rows // 2
    everything = (0, chunk_rows)
    up_groups = [(hops + above + 1, hops + above + 1, (0, part))] if shared else []
    up_groups += [(max(top - GROUP + 1, 1), top, everything) for top in range(hops + above, 0, -GROUP)]
    down_groups = [(-below - 1, -below - 1, (part, part))] if shared else []
    down_groups += [(low, min(low + GROUP - 1, hops - 1), everything) for low in range(-below, hops, GROUP)]
    upward, downward = chip(1), chip(-1)

    def up_range(j, g):
        low, top, held = up_groups[g]
        low = max(low, j + 1)
        return (low - j, top - low + 1, held) if low <= top else None

    def down_range(j, g):
        low, top, held = down_groups[g]
        top = min(top, j - 1)
        return (low - j, top - low + 1, held) if low <= top else None

    def send_up(j, g):
        found = up_range(j, g)
        if found is None or j == hops:
            return
        e, count, held = found
        held = pl.ds(*held)
        src = partial.at[0, pl.ds(e, count), held] if j == 0 else up.at[j - 1, pl.ds(e, count), held]
        send(src, up.at[j, pl.ds(e - 1, count), held], up_send.at[j, g], up_recv.at[j, g], upward)

    def send_down(j, g):
        found = down_range(j, g)
        if found is None or j == 0:
            return
        e, count, held = found
        held = pl.ds(*held)
        src = (partial.at[hops] if j == hops else down.at[j]).at[pl.ds(e + ring, count), held]
        dst = down.at[j - 1, pl.ds(e + 1 + ring, count), held]
        send(src, dst, down_send.at[j - 1, g], down_recv.at[j - 1, g], downward)

    most = max(len(up_groups), len(down_groups))
    for g in range(most):
        if g < len(up_groups):
            send_up(0, g)
        if g < len(down_groups):
            send_down(hops, g)

    contributions(1)

    per_owner = chunk_rows // rows

    def deliver(total, slot, j, e, start=0):
        owners = range(start // per_owner, (start + total.shape[0]) // per_owner)
        for a in owners:
            piece = total[a * per_owner - start : (a + 1) * per_owner - start]
            ready[slot, a] = jnp.concatenate([piece[:, :LANES], piece[:, LANES:]], axis=0)
        dst = landed.at[lax.rem(here - j + blocks, blocks)]
        for d in owners:
            if e:
                where = {"tm_0": d, "tm_1": lax.rem(z + e + ring, ring)}
                send(ready.at[slot, d], dst, last_send.at[slot, d], last_recv, where)
                continue
            owner = lax.rem(x + d, rows)
            src = ready.at[slot, owner]
            if d == 0:
                pltpu.make_async_copy(src, dst, last_recv).start()
            else:
                send(src, dst, last_send.at[slot, d], last_recv, {"tm_0": owner})

    def wait_for(ref, sem):
        pltpu.make_async_copy(ref, ref, sem).wait()

    def arrive_up(j, g):
        arrived = up_range(j - 1, g)
        if arrived is None:
            return
        e, count, held = arrived
        e, span = e - 1, pl.ds(*held)
        wait_for(up.at[j - 1, pl.ds(e, count), span], up_recv.at[j - 1, g])
        for c in range(e, e + count):
            if c > 0:
                total = up[j - 1, c, span] + partial[j, c, span]
                if j < hops:
                    up[j - 1, c, span] = total
                else:
                    deliver(total, c + hops + below, j, c, held[0])
        send_up(j, g)

    def arrive_down(i, g):
        arrived = down_range(i + 1, g)
        if arrived is None:
            return
        e, count, held = arrived
        e, span = e + 1, pl.ds(*held)
        wait_for(down.at[i, pl.ds(e + ring, count), span], down_recv.at[i, g])
        for c in range(e, e + count):
            if c < 0:
                total = down[i, c + ring, span] + partial[i, c + ring, span]
                if i > 0:
                    down[i, c + ring, span] = total
                else:
                    deliver(total, (c + below + ring) % ring, 0, c, held[0])
        send_down(i, g)

    def template_spectra():
        templ_copy.wait()
        for copy in table_copies[:3]:
            copy.wait()
        count = out_ref.shape[1]
        short = templ_ref.shape[0] // count
        templates = [templ_ref[pl.ds(i, short, stride=count), :] for i in range(count)]
        templ_spec[...] = forward(templates, first_half_ref[...], twiddle_ref[...], second_ref[...])
        for i in range(count):
            energy = jnp.sqrt(jnp.sum(templates[i] * templates[i], keepdims=True) + 1e-06)
            gain[pl.ds(i, 1), :] = jnp.broadcast_to(1.0 / (scale * energy), (1, LANES))

    for step in range(1, hops + 1):
        j, i = step, hops - step
        for g in range(most):
            if g < len(up_groups):
                arrive_up(j, g)
            if g < len(down_groups):
                arrive_down(i, g)
            if g == min(2, most - 1):
                if step + 1 <= hops // 2:
                    contributions(step + 1)
                elif step == hops // 2:
                    template_spectra()
        for at in [j, i] if j > i else [j] if j == i else []:
            total = partial[at, 0]
            if at > 0:
                total = total + up[at - 1, 0]
            if at < hops:
                total = total + down[at, ring]
            deliver(total, at + below, at, 0)

    for swap in swaps:
        swap.wait_send()
    for copy in sends:
        copy.wait_send()
    for copy in table_copies[3:]:
        copy.wait()
    wait_for(landed, last_recv)

    count = out_ref.shape[1]
    long = blocks * 2
    flat = landed.reshape(long * count, LANES)
    half = twiddle_ref.shape[1]
    series = [flat[pl.ds(i, long, stride=count), :] for i in range(count)]
    twiddle = twiddle_ref[...]
    spec = forward(series, first_ref[...], twiddle, second_ref[...])
    sr, si, hr, hi = spec[:, :LANES], spec[:, LANES:], templ_spec[:, :LANES], templ_spec[:, LANES:]
    product = jnp.concatenate([sr * hr + si * hi, si * hr - sr * hi], axis=1)
    back = dot3(split(product), (third_ref[0], third_ref[1]))
    for i in range(count):
        re, im = back[i * half : (i + 1) * half, :LANES], back[i * half : (i + 1) * half, LANES:]
        turned = jnp.concatenate([re * twiddle[0] + im * twiddle[1], im * twiddle[0] - re * twiddle[1]], axis=0)
        lags = dot3((fourth_ref[0], fourth_ref[1]), split(turned))
        out_ref[:, i, :] = lags * gain[pl.ds(i, 1), :]


def fourier_tables(length, lag_count):
    blocks = length // LANES
    kept = blocks // 2 + 1
    half = -(-kept // 8) * 8
    f1 = np.arange(half)
    n1 = np.arange(blocks)
    n2 = np.arange(LANES)
    live = (f1 < kept)[:, None]
    angle = 2.0 * np.pi * ((f1[:, None] * n1[None, :]) % blocks) / blocks
    first = np.concatenate([np.cos(angle) * live, -np.sin(angle) * live])
    turn = 2.0 * np.pi * ((f1[:, None] * n2[None, :]) % length) / length
    twiddle = np.stack([np.cos(turn) * live, -np.sin(turn) * live]).astype(np.float32)
    inner = 2.0 * np.pi * ((n2[:, None] * n2[None, :]) % LANES) / LANES
    c, s = np.cos(inner), np.sin(inner)
    second = np.block([[c, -s], [s, c]])
    third = np.block([[c, s], [-s, c]])
    weight = np.where((f1 == 0) | (f1 == kept - 1), 1.0, 2.0) * (f1 < kept) / length
    lag_rows = lag_count // LANES
    back = angle.T[:lag_rows]
    fourth = np.concatenate([np.cos(back) * weight, -np.sin(back) * weight], axis=1)
    return (
        split_constant(first),
        split_constant(first[:, :lag_rows]),
        jnp.asarray(twiddle),
        split_constant(second),
        split_constant(third),
        split_constant(fourth),
    )


def on_device(traces, templates, moveouts, masks):
    rows, ring = lax.axis_size("tm_0"), lax.axis_size("tm_1")
    channels, samples = traces.shape
    length = samples * rows * ring * 2
    count, lag_count = templates.shape
    chip_samples = 2 * samples
    hops = (length // 8) // chip_samples
    outside = ring - 1 - hops
    above = below = outside // 2
    shared = outside % 2
    cfg = (rows, ring, hops, above, below, shared)
    chunk = (rows * count, chip_samples)
    lag_rows = lag_count // LANES
    tiles = templates.reshape(count, lag_rows, LANES).transpose(1, 0, 2).reshape(lag_rows * count, LANES)
    tables = fourier_tables(length, lag_count)
    groups = -(-(hops + above) // GROUP) + shared
    vmem = pl.BlockSpec(memory_space=pltpu.VMEM)
    anywhere = pl.BlockSpec(memory_space=pl.ANY)
    dma = pltpu.SemaphoreType.DMA
    half = tables[2].shape[1]
    found = pl.pallas_call(
        functools.partial(matched_kernel, cfg, math.sqrt(channels)),
        out_shape=jax.ShapeDtypeStruct((lag_rows, count, LANES), jnp.float32),
        in_specs=[anywhere] * (4 + len(tables)),
        out_specs=vmem,
        scratch_shapes=[
            pltpu.VMEM((channels, samples), jnp.float32),
            pltpu.VMEM((channels // LANES, LANES), jnp.int32),
            pltpu.VMEM((2, channels, samples), jnp.float32),
            pltpu.VMEM((rows, ring, 2 * count, channels), jnp.int32),
            pltpu.VMEM((ring, rows * count, channels), jnp.bfloat16),
            pltpu.VMEM((2, 2, channels, samples), jnp.bfloat16),
            pltpu.VMEM((channels, samples), jnp.bfloat16),
            pltpu.VMEM((2, channels, chip_samples), jnp.bfloat16),
            pltpu.VMEM((hops + 1, ring, *chunk), jnp.float32),
            pltpu.VMEM((hops, ring, *chunk), jnp.float32),
            pltpu.VMEM((hops, ring + 1, *chunk), jnp.float32),
            pltpu.VMEM((ring, rows, 2 * count, LANES), jnp.float32),
            pltpu.VMEM((rows * ring, 2 * count, LANES), jnp.float32),
            pltpu.VMEM(tiles.shape, jnp.float32),
            *[pltpu.VMEM(t.shape, t.dtype) for t in tables],
            pltpu.VMEM((count * half, 2 * LANES), jnp.float32),
            pltpu.VMEM((count, LANES), jnp.float32),
            dma((4 + PIECES + len(tables),)),
            dma((PIECES,)),
            dma((PIECES,)),
            dma((hops, groups)),
            dma((hops, groups)),
            dma((hops, groups)),
            dma((hops, groups)),
            dma((ring, rows)),
            dma,
        ],
        compiler_params=pltpu.CompilerParams(collective_id=0, has_side_effects=True),
    )(
        traces,
        masks.reshape(rows, ring, 2 * count, channels),
        moveouts.reshape(channels // LANES, LANES),
        tiles,
        *tables,
    )
    return found.transpose(1, 0, 2).reshape(count, lag_count)


def solution(mesh):
    finer = Mesh(mesh.devices.reshape(mesh.shape["grp"], 4, -1, 2), ("grp", "tm_0", "tm_1", "tm_2"))
    axes = ("tm_0", "tm_1", "tm_2")
    return jax.shard_map(
        on_device,
        mesh=finer,
        in_specs=(P("grp", axes), P(axes, None), P("grp"), P(None, "grp")),
        out_specs=P(axes, "grp"),
        check_vma=False,
    )
```

time: 81.6 us -> 75.7 us (0.928)
  Pallas kernels: 81.4 us -> 74 us
  local copies, waits for them, and re-layouts: 0 us -> 1.57 us
    pallas_call x2 -> x1, Pallas kernels: 81.4 us -> 74 us  [on_device(): pl.pallas_call(functools.partial(matched_kernel, cfg, math.sqrt(channels)...]
    unnamed x0 -> x1, local copies, waits for them, and re-layouts: none -> 1.57 us
where the time goes in v1:
time: 75.7 us; the launch traced here: 75.5 us
  Pallas kernels  74 us (98%)
  local copies, waits for them, and re-layouts  1.57 us (2%)
    pallas_call x1, Pallas kernels, on_device(): pl.pallas_call(functools.partial(matched_kernel, cfg, math.sqrt(channels)...  74 us
    unnamed x1, local copies, waits for them, and re-layouts  1.57 us

profile of v1, /device:TPU:40, one launch (start us, length us, event | category | flops | bytes accessed | tf_op | source)
XLA Modules:
  0.0 75.5 jit_solution(2615919363562586637)
XLA Ops:
  0.0 74.0 %shard_map.100 = f32[64,4,128]{2,1,0:T(4,128)} custom-call(f32[1024,128]{1,0:T(8,128)} %x_hbm.1, s32[4,16,8,1024]{3,2,1,0:T(8,128)} %bitcast.10, s32[8,128]{1,0:T(8,128)} %bitcast.13, f32[256,128]{1,0:T(8,128)} %bitcast.12, bf16[2,144,128]{2,1,0:T(8,128)(2,1)} %constant.12.clone.first_hbm, bf16[2,144,64]{2,1,0:T(8,128)(2,1)} %constant.13.clone.first_half_hbm, ...), custom_call_target="tpu_custom_call" | custom-call | tf_op jit(solution)/shard_map/pallas_call | solution.py:414
  74.0 1.6 %copy.13 = f32[4,8192]{1,0:T(4,128)} copy(f32[4,8192]{1,0:T(4,128)} %bitcast.11) | data formatting | bytes 262144

commit v2 on v1

--- a/solution.py
+++ b/solution.py
@@ -12,7 +12,7 @@
 
 MESH = pl.DeviceIdType.MESH
 LANES = 128
-GROUP = 2
+GROUP = 1
 PIECES = 4
 
 
@@ -85,14 +85,9 @@
 
     barrier = pltpu.get_barrier_semaphore()
     pl.semaphore_signal(barrier, inc=1, device_id=partner, device_id_type=MESH)
-    senders = 1
-    reach = max(above, below) + shared
-    for dz in range(-reach, reach + 1):
-        for dx in range(rows):
-            if dx or dz:
-                where = {"tm_0": lax.rem(x + dx, rows), "tm_1": lax.rem(z + dz + ring, ring)}
-                pl.semaphore_signal(barrier, inc=1, device_id=where, device_id_type=MESH)
-                senders += 1
+    peers = [chip(1), chip(-1)] + [{"tm_0": lax.rem(x + d, rows)} for d in range(1, rows)]
+    for where in peers:
+        pl.semaphore_signal(barrier, inc=1, device_id=where, device_id_type=MESH)
 
     mask_copy = load(masks_hbm, mask_int)
     templ_copy = load(templ_hbm, templ_ref)
@@ -126,7 +121,7 @@
             halves[1, core, at, :] = low
 
         if p == 0:
-            pl.semaphore_wait(barrier, senders)
+            pl.semaphore_wait(barrier, 1 + len(peers))
         half = pair.at[core, pl.ds(p * per_piece, per_piece)]
         swap = pltpu.make_async_remote_copy(
             src_ref=half, dst_ref=half, send_sem=pair_send.at[p], recv_sem=pair_recv.at[p],
@@ -193,14 +188,17 @@
 
     contributions(0)
 
-    sends = []
-
-    def send(src, dst, send_sem, recv_sem, where):
-        copy = pltpu.make_async_remote_copy(
+    sent = {"up": 0, "down": 0, "last": 0}
+    slots = {"up": {}, "down": {}}
+
+    def slot_of(name, j, g):
+        return slots[name].setdefault((j, g), len(slots[name]))
+
+    def send(name, src, dst, send_sem, recv_sem, where):
+        pltpu.make_async_remote_copy(
             src_ref=src, dst_ref=dst, send_sem=send_sem, recv_sem=recv_sem, device_id=where, device_id_type=MESH
-        )
-        copy.start()
-        sends.append(copy)
+        ).start()
+        sent[name] += math.prod(src.shape)
 
     chunk_rows = partial.shape[2]
     part = chunk_rows // 2
@@ -228,7 +226,7 @@
         e, count, held = found
         held = pl.ds(*held)
         src = partial.at[0, pl.ds(e, count), held] if j == 0 else up.at[j - 1, pl.ds(e, count), held]
-        send(src, up.at[j, pl.ds(e - 1, count), held], up_send.at[j, g], up_recv.at[j, g], upward)
+        send("up", src, up.at[j, pl.ds(e - 1, count), held], up_send, up_recv.at[slot_of("up", j, g)], upward)
 
     def send_down(j, g):
         found = down_range(j, g)
@@ -238,7 +236,7 @@
         held = pl.ds(*held)
         src = (partial.at[hops] if j == hops else down.at[j]).at[pl.ds(e + ring, count), held]
         dst = down.at[j - 1, pl.ds(e + 1 + ring, count), held]
-        send(src, dst, down_send.at[j - 1, g], down_recv.at[j - 1, g], downward)
+        send("down", src, dst, down_send, down_recv.at[slot_of("down", j - 1, g)], downward)
 
     most = max(len(up_groups), len(down_groups))
     for g in range(most):
@@ -248,61 +246,6 @@
             send_down(hops, g)
 
     contributions(1)
-
-    per_owner = chunk_rows // rows
-
-    def deliver(total, slot, j, e, start=0):
-        owners = range(start // per_owner, (start + total.shape[0]) // per_owner)
-        for a in owners:
-            piece = total[a * per_owner - start : (a + 1) * per_owner - start]
-            ready[slot, a] = jnp.concatenate([piece[:, :LANES], piece[:, LANES:]], axis=0)
-        dst = landed.at[lax.rem(here - j + blocks, blocks)]
-        for d in owners:
-            if e:
-                where = {"tm_0": d, "tm_1": lax.rem(z + e + ring, ring)}
-                send(ready.at[slot, d], dst, last_send.at[slot, d], last_recv, where)
-                continue
-            owner = lax.rem(x + d, rows)
-            src = ready.at[slot, owner]
-            if d == 0:
-                pltpu.make_async_copy(src, dst, last_recv).start()
-            else:
-                send(src, dst, last_send.at[slot, d], last_recv, {"tm_0": owner})
-
-    def wait_for(ref, sem):
-        pltpu.make_async_copy(ref, ref, sem).wait()
-
-    def arrive_up(j, g):
-        arrived = up_range(j - 1, g)
-        if arrived is None:
-            return
-        e, count, held = arrived
-        e, span = e - 1, pl.ds(*held)
-        wait_for(up.at[j - 1, pl.ds(e, count), span], up_recv.at[j - 1, g])
-        for c in range(e, e + count):
-            if c > 0:
-                total = up[j - 1, c, span] + partial[j, c, span]
-                if j < hops:
-                    up[j - 1, c, span] = total
-                else:
-                    deliver(total, c + hops + below, j, c, held[0])
-        send_up(j, g)
-
-    def arrive_down(i, g):
-        arrived = down_range(i + 1, g)
-        if arrived is None:
-            return
-        e, count, held = arrived
-        e, span = e + 1, pl.ds(*held)
-        wait_for(down.at[i, pl.ds(e + ring, count), span], down_recv.at[i, g])
-        for c in range(e, e + count):
-            if c < 0:
-                total = down[i, c + ring, span] + partial[i, c + ring, span]
-                if i > 0:
-                    down[i, c + ring, span] = total
-                else:
-                    deliver(total, (c + below + ring) % ring, 0, c, held[0])
-        send_down(i, g)
 
     def template_spectra():
         templ_copy.wait()
@@ -316,6 +259,63 @@
             energy = jnp.sqrt(jnp.sum(templates[i] * templates[i], keepdims=True) + 1e-06)
             gain[pl.ds(i, 1), :] = jnp.broadcast_to(1.0 / (scale * energy), (1, LANES))
 
+    template_spectra()
+
+    per_owner = chunk_rows // rows
+
+    def deliver(total, slot, j, e, start=0):
+        owners = range(start // per_owner, (start + total.shape[0]) // per_owner)
+        for a in owners:
+            piece = total[a * per_owner - start : (a + 1) * per_owner - start]
+            ready[slot, a] = jnp.concatenate([piece[:, :LANES], piece[:, LANES:]], axis=0)
+        dst = landed.at[lax.rem(here - j + blocks, blocks)]
+        for d in owners:
+            if e:
+                where = {"tm_0": d, "tm_1": lax.rem(z + e + ring, ring)}
+                send("last", ready.at[slot, d], dst, last_send, last_recv, where)
+                continue
+            owner = lax.rem(x + d, rows)
+            src = ready.at[slot, owner]
+            if d == 0:
+                pltpu.make_async_copy(src, dst, last_recv).start()
+            else:
+                send("last", src, dst, last_send, last_recv, {"tm_0": owner})
+
+    def wait_for(ref, sem):
+        pltpu.make_async_copy(ref, ref, sem).wait()
+
+    def arrive_up(j, g):
+        arrived = up_range(j - 1, g)
+        if arrived is None:
+            return
+        e, count, held = arrived
+        e, span = e - 1, pl.ds(*held)
+        wait_for(up.at[j - 1, pl.ds(e, count), span], up_recv.at[slot_of("up", j - 1, g)])
+        for c in range(e, e + count):
+            if c > 0:
+                total = up[j - 1, c, span] + partial[j, c, span]
+                if j < hops:
+                    up[j - 1, c, span] = total
+                else:
+                    deliver(total, c + hops + below, j, c, held[0])
+        send_up(j, g)
+
+    def arrive_down(i, g):
+        arrived = down_range(i + 1, g)
+        if arrived is None:
+            return
+        e, count, held = arrived
+        e, span = e + 1, pl.ds(*held)
+        wait_for(down.at[i, pl.ds(e + ring, count), span], down_recv.at[slot_of("down", i, g)])
+        for c in range(e, e + count):
+            if c < 0:
+                total = down[i, c + ring, span] + partial[i, c + ring, span]
+                if i > 0:
+                    down[i, c + ring, span] = total
+                else:
+                    deliver(total, (c + below + ring) % ring, 0, c, held[0])
+        send_down(i, g)
+
     for step in range(1, hops + 1):
         j, i = step, hops - step
         for g in range(most):
@@ -326,8 +326,6 @@
             if g == min(2, most - 1):
                 if step + 1 <= hops // 2:
                     contributions(step + 1)
-                elif step == hops // 2:
-                    template_spectra()
         for at in [j, i] if j > i else [j] if j == i else []:
             total = partial[at, 0]
             if at > 0:
@@ -338,8 +336,11 @@
 
     for swap in swaps:
         swap.wait_send()
-    for copy in sends:
-        copy.wait_send()
+    chunk = math.prod(partial.shape[2:])
+    stripes = (hops * ring, *partial.shape[2:])
+    wait_for(up.reshape(stripes).at[pl.ds(0, sent["up"] // chunk)], up_send)
+    wait_for(up.reshape(stripes).at[pl.ds(0, sent["down"] // chunk)], down_send)
+    wait_for(landed.at[pl.ds(0, sent["last"] // math.prod(landed.shape[1:]))], last_send)
     for copy in table_copies[3:]:
         copy.wait()
     wait_for(landed, last_recv)
@@ -406,7 +407,7 @@
     lag_rows = lag_count // LANES
     tiles = templates.reshape(count, lag_rows, LANES).transpose(1, 0, 2).reshape(lag_rows * count, LANES)
     tables = fourier_tables(length, lag_count)
-    groups = -(-(hops + above) // GROUP) + shared
+    messages = sum(min(top, hops) for top in range(hops + above, 0, -GROUP)) + shared * hops
     vmem = pl.BlockSpec(memory_space=pltpu.VMEM)
     anywhere = pl.BlockSpec(memory_space=pl.ANY)
     dma = pltpu.SemaphoreType.DMA
@@ -437,11 +438,11 @@
             dma((4 + PIECES + len(tables),)),
             dma((PIECES,)),
             dma((PIECES,)),
-            dma((hops, groups)),
-            dma((hops, groups)),
-            dma((hops, groups)),
-            dma((hops, groups)),
-            dma((ring, rows)),
+            dma,
+            dma((messages,)),
+            dma,
+            dma((messages,)),
+            dma,
             dma,
         ],
         compiler_params=pltpu.CompilerParams(collective_id=0, has_side_effects=True),

time: 75.7 us -> 73.6 us (0.972)
  Pallas kernels: 74 us -> 71.9 us
    pallas_call x1, Pallas kernels: 74 us -> 71.9 us  [on_device(): pl.pallas_call(functools.partial(matched_kernel, cfg, math.sqrt(channels)...]
where the time goes in v2:
time: 73.6 us; the launch traced here: 73.5 us
  Pallas kernels  71.9 us (98%)
  local copies, waits for them, and re-layouts  1.57 us (2%)
    pallas_call x1, Pallas kernels, on_device(): pl.pallas_call(functools.partial(matched_kernel, cfg, math.sqrt(channels)...  71.9 us
    unnamed x1, local copies, waits for them, and re-layouts  1.57 us

profile of v2, /device:TPU:40, one launch (start us, length us, event | category | flops | bytes accessed | tf_op | source)
XLA Modules:
  0.0 73.5 jit_solution(12290646113340991440)
XLA Ops:
  0.0 71.9 %shard_map.100 = f32[64,4,128]{2,1,0:T(4,128)} custom-call(f32[1024,128]{1,0:T(8,128)} %x_hbm.1, s32[4,16,8,1024]{3,2,1,0:T(8,128)} %bitcast.10, s32[8,128]{1,0:T(8,128)} %bitcast.13, f32[256,128]{1,0:T(8,128)} %bitcast.12, bf16[2,144,128]{2,1,0:T(8,128)(2,1)} %constant.12.clone.first_hbm, bf16[2,144,64]{2,1,0:T(8,128)(2,1)} %constant.13.clone.first_half_hbm, ...), custom_call_target="tpu_custom_call" | custom-call | tf_op jit(solution)/shard_map/pallas_call | solution.py:415
  71.9 1.6 %copy.13 = f32[4,8192]{1,0:T(4,128)} copy(f32[4,8192]{1,0:T(4,128)} %bitcast.11) | data formatting | bytes 262144

commit v3 on v2

v3 whole, which is shorter than its diff:
```python
import functools
import math

import jax
import jax.numpy as jnp
import numpy as np
from jax import lax
from jax.experimental import pallas as pl
from jax.experimental.pallas import tpu as pltpu
from jax.sharding import Mesh
from jax.sharding import PartitionSpec as P

MESH = pl.DeviceIdType.MESH
LANES = 128
GROUP = 1
PIECES = 4


def split(value):
    high = value.astype(jnp.bfloat16)
    low = (value - high.astype(jnp.float32)).astype(jnp.bfloat16)
    return high, low


def split_constant(value):
    value = np.asarray(value, np.float64).astype(np.float32)
    high = value.astype(jnp.bfloat16)
    low = (value - high.astype(np.float32)).astype(jnp.bfloat16)
    return jnp.asarray(np.stack([high, low]))


def mm(a, b):
    return jnp.dot(a, b, preferred_element_type=jnp.float32)


def dot3(left, right):
    (left_hi, left_lo), (right_hi, right_lo) = left, right
    return mm(left_hi, right_hi) + (mm(left_hi, right_lo) + mm(left_lo, right_hi))


def forward(series, first, twiddle, second):
    half = twiddle.shape[1]
    turned = []
    for s in series:
        y = dot3((first[0], first[1]), split(s))
        re, im = y[:half], y[half:]
        turned.append(
            jnp.concatenate([re * twiddle[0] - im * twiddle[1], re * twiddle[1] + im * twiddle[0]], axis=1)
        )
    return dot3(split(jnp.concatenate(turned, axis=0)), (second[0], second[1]))


def matched_kernel(
    cfg, scale,
    x_hbm, masks_hbm, mo_hbm, templ_hbm, first_hbm, first_half_hbm, twiddle_hbm, second_hbm, third_hbm, fourth_hbm,
    out_ref,
    raw, mo_ref, pair, mask_int, mask_rows, halves, shift_at, parts, partial, flow, merge, ready, landed,
    templ_ref, first_ref, first_half_ref, twiddle_ref, second_ref, third_ref, fourth_ref, templ_spec, gain,
    load_sem, pair_send, pair_recv, flow_send, flow_recv, merge_send, merge_recv, last_send, last_recv,
):
    rows, ring, hops, outside, shared = cfg
    channels = x_hbm.shape[0]
    blocks = rows * ring
    x = lax.axis_index("tm_0")
    z = lax.axis_index("tm_1")
    core = lax.axis_index("tm_2")
    toward = 1 - 2 * core
    here = x * ring + z
    partner = {"tm_2": 1 - core}

    def chip(step):
        other = lax.rem(here + step + blocks, blocks)
        return {"tm_0": other // ring, "tm_1": lax.rem(other, ring)}

    def window_place(s):
        return core * hops + toward * s

    def wait_for(ref, sem):
        pltpu.make_async_copy(ref, ref, sem).wait()

    loads = []

    def load(src, dst):
        copy = pltpu.make_async_copy(src, dst, load_sem.at[len(loads)])
        copy.start()
        loads.append(copy)
        return copy

    per_piece = channels // PIECES
    mo_copy = load(mo_hbm, mo_ref)
    x_copies = [load(x_hbm.at[pl.ds(p * per_piece, per_piece)], raw.at[pl.ds(p * per_piece, per_piece)]) for p in range(PIECES)]

    barrier = pltpu.get_barrier_semaphore()
    peers = [partner, chip(1), chip(-1)]
    for d in range(1, rows):
        peers += [{"tm_0": lax.rem(x + d, rows), "tm_2": c} for c in (core, 1 - core)]
    for where in peers:
        pl.semaphore_signal(barrier, inc=1, device_id=where, device_id_type=MESH)

    mask_copy = load(masks_hbm, mask_int)
    templ_copy = load(templ_hbm, templ_ref)
    table_copies = [
        load(first_half_hbm, first_half_ref),
        load(twiddle_hbm, twiddle_ref),
        load(second_hbm, second_ref),
        load(first_hbm, first_ref),
        load(third_hbm, third_ref),
        load(fourth_hbm, fourth_ref),
    ]

    lane = lax.broadcasted_iota(jnp.int32, (LANES, LANES), 1)
    mo_copy.wait()
    swaps = []
    for p in range(PIECES):
        x_copies[p].wait()

        @pl.loop(p * per_piece // LANES, (p + 1) * per_piece // LANES)
        def _(b):
            at = pl.ds(pl.multiple_of(b * LANES, LANES), LANES)
            spread = jnp.broadcast_to(mo_ref[pl.ds(b, 1), :].astype(jnp.float32), (LANES, LANES))
            move = jnp.transpose(spread).astype(jnp.int32)
            index = lane + (move & (LANES - 1))
            value = jnp.take_along_axis(raw[at, :], index & (LANES - 1), axis=1)
            pair[core, at, :] = value
            passed = (index >= LANES).astype(jnp.int32)
            shift_at[at, :] = ((move >> (LANES.bit_length() - 1)) + passed).astype(jnp.float32).astype(jnp.bfloat16)
            high, low = split(value)
            halves[0, core, at, :] = high
            halves[1, core, at, :] = low

        if p == 0:
            pl.semaphore_wait(barrier, len(peers))
        half = pair.at[core, pl.ds(p * per_piece, per_piece)]
        swap = pltpu.make_async_remote_copy(
            src_ref=half, dst_ref=half, send_sem=pair_send.at[p], recv_sem=pair_recv.at[p],
            device_id=partner, device_id_type=MESH,
        )
        swap.start()
        swaps.append(swap)

    mask_copy.wait()
    tile_rows = mask_int.shape[2]
    per_owner = tile_rows // 2
    own_rows = rows * per_owner
    chunk_rows = 2 * own_rows
    tops = lax.broadcasted_iota(jnp.int32, (tile_rows, channels), 0) < per_owner

    def pick(first, second, side):
        moved = pltpu.roll(jnp.where(side == 0, second, first), per_owner, 0)
        kept = jnp.where(side == 0, first, second)
        return jnp.where(tops == (side == 0), kept, moved).astype(jnp.float32)

    @pl.loop(0, mask_rows.shape[0])
    def _(m):
        owner = lax.rem(z + toward * m + ring, ring)
        tiles = [mask_int[a, owner] for a in range(rows)]
        pieces = [pick(tiles[a], tiles[a + 1], side) for side in (core, 1 - core) for a in range(0, rows, 2)]
        mask_rows[m] = jnp.concatenate(pieces, axis=0).astype(jnp.bfloat16)

    for p in range(PIECES):
        swaps[p].wait_recv()

        @pl.loop(p * per_piece // LANES, (p + 1) * per_piece // LANES)
        def _(b):
            at = pl.ds(pl.multiple_of(b * LANES, LANES), LANES)
            high, low = split(pair[1 - core, at, :])
            halves[0, 1 - core, at, :] = high
            halves[1, 1 - core, at, :] = low

    zero = jnp.zeros((LANES, LANES), jnp.bfloat16)
    top = hops + outside

    def contribution(s):
        twice = jnp.broadcast_to((2 * window_place(s)).astype(jnp.float32), (LANES, LANES))
        before, same, after = ((twice + d).astype(jnp.bfloat16) for d in (-1, 0, 1))

        @pl.loop(0, channels // LANES)
        def _(b):
            at = pl.ds(pl.multiple_of(b * LANES, LANES), LANES)
            shift = shift_at[at, :]
            is_before, is_same, is_after = shift == before, shift == same, shift == after
            for t in range(2):
                first, second = halves[t, 0, at, :], halves[t, 1, at, :]
                parts[t, at, :LANES] = jnp.where(is_same, first, jnp.where(is_after, second, zero))
                parts[t, at, LANES:] = jnp.where(is_before, first, jnp.where(is_same, second, zero))

        full = top - s + 1
        weights = mask_rows[pl.ds(0, full)].reshape(full * chunk_rows, channels)
        if shared:
            weights = jnp.concatenate([weights, mask_rows[full, pl.ds(0, own_rows)]], axis=0)
        total = mm(weights, parts[0]) + mm(weights, parts[1])
        partial[s, pl.ds(0, full)] = total[: full * chunk_rows].reshape(full, chunk_rows, 2 * LANES)
        if shared:
            partial[s, full, pl.ds(0, own_rows)] = total[full * chunk_rows :]

    contribution(0)

    sent = {"flow": 0, "merge": 0, "last": 0}
    slots = {}

    def slot_of(s, g):
        return slots.setdefault((s, g), len(slots))

    def send(name, src, dst, send_sem, recv_sem, where):
        pltpu.make_async_remote_copy(
            src_ref=src, dst_ref=dst, send_sem=send_sem, recv_sem=recv_sem, device_id=where, device_id_type=MESH
        ).start()
        sent[name] += math.prod(src.shape)

    groups = [(top + 1, top + 1, own_rows)] if shared else []
    groups += [(max(high - GROUP + 1, 1), high, chunk_rows) for high in range(top, 0, -GROUP)]
    onward = chip(toward)

    def span(s, g):
        low, high, held = groups[g]
        low = max(low, s + 1)
        return (low - s, high - low + 1, pl.ds(0, held)) if low <= high and s < hops else None

    def send_on(s, g):
        found = span(s, g)
        if found is None:
            return
        m, count, held = found
        src = partial.at[0, pl.ds(m, count), held] if s == 0 else flow.at[s - 1, pl.ds(m, count), held]
        dst = flow.at[s, pl.ds(m - 1, count), held]
        send("flow", src, dst, flow_send, flow_recv.at[slot_of(s, g)], onward)

    for g in range(len(groups)):
        send_on(0, g)

    def template_spectra():
        templ_copy.wait()
        for copy in table_copies[:3]:
            copy.wait()
        count = out_ref.shape[1]
        short = templ_ref.shape[0] // count
        templates = [templ_ref[pl.ds(i, short, stride=count), :] for i in range(count)]
        templ_spec[...] = forward(templates, first_half_ref[...], twiddle_ref[...], second_ref[...])
        for i in range(count):
            energy = jnp.sqrt(jnp.sum(templates[i] * templates[i], keepdims=True) + 1e-06)
            gain[pl.ds(i, 1), :] = jnp.broadcast_to(1.0 / (scale * energy), (1, LANES))

    contribution(1)
    contribution(2)
    template_spectra()
    todo = list(range(3, hops + 1))

    def deliver(total, s, m, sides):
        slot = s + m
        for side in range(sides):
            for a in range(rows):
                start = side * own_rows + a * per_owner
                piece = total[start : start + per_owner]
                ready[slot, side, a] = jnp.concatenate([piece[:, :LANES], piece[:, LANES:]], axis=0)
        dst = landed.at[lax.rem(here - window_place(s) + blocks, blocks)]
        for side in range(sides):
            cores = core if side == 0 else 1 - core
            for d in range(rows):
                if m:
                    src, where = ready.at[slot, side, d], {"tm_0": d, "tm_1": lax.rem(z + toward * m + ring, ring)}
                else:
                    owner = lax.rem(x + d, rows)
                    src, where = ready.at[slot, side, owner], {"tm_0": owner}
                if m == 0 and side == 0 and d == 0:
                    pltpu.make_async_copy(src, dst, last_recv).start()
                else:
                    send("last", src, dst, last_send, last_recv, {**where, "tm_2": cores})

    def merge_and_deliver(s):
        wait_for(merge.at[s], merge_recv.at[s])
        own = pl.ds(0, own_rows)
        deliver(flow[s - 1, 0, own] + partial[s, 0, own] + merge[s], s, 0, 1)

    def arrive(s, g):
        arrived = span(s - 1, g)
        if arrived is None:
            return
        m, count, held = arrived
        m = m - 1
        wait_for(flow.at[s - 1, pl.ds(m, count), held], flow_recv.at[slot_of(s - 1, g)])
        for c in reversed(range(m, m + count)):
            if s == hops:
                deliver(flow[s - 1, c, held] + partial[s, c, held], s, c, held.size // own_rows)
            elif c > 0:
                flow[s - 1, c, held] = flow[s - 1, c, held] + partial[s, c, held]
            else:
                src = flow.at[s - 1, 0, pl.ds(own_rows, own_rows)]
                send("merge", src, merge.at[hops - s], merge_send, merge_recv.at[hops - s], partner)
        send_on(s, g)

    for s in range(1, hops + 1):
        if s == hops and hops % 2 == 0:
            merge_and_deliver(hops // 2)
        for g in range(len(groups)):
            arrive(s, g)
            if todo and g in (2, 6):
                contribution(todo.pop(0))
        if hops < 2 * s < 2 * hops:
            merge_and_deliver(s)
    for s in range((hops - 1) // 2, 0, -1):
        merge_and_deliver(s)

    for swap in swaps:
        swap.wait_send()
    wait_for(flow.reshape(-1, chunk_rows, 2 * LANES).at[pl.ds(0, sent["flow"] // math.prod(flow.shape[2:]))], flow_send)
    wait_for(merge.at[pl.ds(0, sent["merge"] // math.prod(merge.shape[1:]))], merge_send)
    wait_for(landed.at[pl.ds(0, sent["last"] // math.prod(landed.shape[1:]))], last_send)
    for copy in table_copies[3:]:
        copy.wait()
    wait_for(landed, last_recv)

    count = out_ref.shape[1]
    long = blocks * 2
    flat = landed.reshape(long * count, LANES)
    half = twiddle_ref.shape[1]
    series = [flat[pl.ds(i, long, stride=count), :] for i in range(count)]
    twiddle = twiddle_ref[...]
    spec = forward(series, first_ref[...], twiddle, second_ref[...])
    sr, si, hr, hi = spec[:, :LANES], spec[:, LANES:], templ_spec[:, :LANES], templ_spec[:, LANES:]
    product = jnp.concatenate([sr * hr + si * hi, si * hr - sr * hi], axis=1)
    back = dot3(split(product), (third_ref[0], third_ref[1]))
    for i in range(count):
        re, im = back[i * half : (i + 1) * half, :LANES], back[i * half : (i + 1) * half, LANES:]
        turned = jnp.concatenate([re * twiddle[0] + im * twiddle[1], im * twiddle[0] - re * twiddle[1]], axis=0)
        lags = dot3((fourth_ref[0], fourth_ref[1]), split(turned))
        out_ref[:, i, :] = lags * gain[pl.ds(i, 1), :]


def fourier_tables(length, lag_count):
    blocks = length // LANES
    kept = blocks // 2 + 1
    half = -(-kept // 8) * 8
    f1 = np.arange(half)
    n1 = np.arange(blocks)
    n2 = np.arange(LANES)
    live = (f1 < kept)[:, None]
    angle = 2.0 * np.pi * ((f1[:, None] * n1[None, :]) % blocks) / blocks
    first = np.concatenate([np.cos(angle) * live, -np.sin(angle) * live])
    turn = 2.0 * np.pi * ((f1[:, None] * n2[None, :]) % length) / length
    twiddle = np.stack([np.cos(turn) * live, -np.sin(turn) * live]).astype(np.float32)
    inner = 2.0 * np.pi * ((n2[:, None] * n2[None, :]) % LANES) / LANES
    c, s = np.cos(inner), np.sin(inner)
    second = np.block([[c, -s], [s, c]])
    third = np.block([[c, s], [-s, c]])
    weight = np.where((f1 == 0) | (f1 == kept - 1), 1.0, 2.0) * (f1 < kept) / length
    lag_rows = lag_count // LANES
    back = angle.T[:lag_rows]
    fourth = np.concatenate([np.cos(back) * weight, -np.sin(back) * weight], axis=1)
    return (
        split_constant(first),
        split_constant(first[:, :lag_rows]),
        jnp.asarray(twiddle),
        split_constant(second),
        split_constant(third),
        split_constant(fourth),
    )


def on_device(traces, templates, moveouts, masks):
    rows, ring = lax.axis_size("tm_0"), lax.axis_size("tm_1")
    channels, samples = traces.shape
    length = samples * rows * ring * 2
    count, lag_count = templates.shape
    chip_samples = 2 * samples
    hops = (length // 8) // chip_samples
    outside, shared = divmod(ring - 1 - hops, 2)
    top = hops + outside
    cfg = (rows, ring, hops, outside, shared)
    chunk = (2 * rows * count, chip_samples)
    lag_rows = lag_count // LANES
    tiles = templates.reshape(count, lag_rows, LANES).transpose(1, 0, 2).reshape(lag_rows * count, LANES)
    tables = fourier_tables(length, lag_count)
    messages = sum(min(high, hops) for high in range(top, 0, -GROUP)) + shared * hops
    vmem = pl.BlockSpec(memory_space=pltpu.VMEM)
    anywhere = pl.BlockSpec(memory_space=pl.ANY)
    dma = pltpu.SemaphoreType.DMA
    half = tables[2].shape[1]
    found = pl.pallas_call(
        functools.partial(matched_kernel, cfg, math.sqrt(channels)),
        out_shape=jax.ShapeDtypeStruct((lag_rows, count, LANES), jnp.float32),
        in_specs=[anywhere] * (4 + len(tables)),
        out_specs=vmem,
        scratch_shapes=[
            pltpu.VMEM((channels, samples), jnp.float32),
            pltpu.VMEM((channels // LANES, LANES), jnp.int32),
            pltpu.VMEM((2, channels, samples), jnp.float32),
            pltpu.VMEM((rows, ring, 2 * count, channels), jnp.int32),
            pltpu.VMEM((top + 1 + shared, 2 * rows * count, channels), jnp.bfloat16),
            pltpu.VMEM((2, 2, channels, samples), jnp.bfloat16),
            pltpu.VMEM((channels, samples), jnp.bfloat16),
            pltpu.VMEM((2, channels, chip_samples), jnp.bfloat16),
            pltpu.VMEM((hops + 1, top + 1 + shared, *chunk), jnp.float32),
            pltpu.VMEM((hops, top + shared, *chunk), jnp.float32),
            pltpu.VMEM((hops, rows * count, chip_samples), jnp.float32),
            pltpu.VMEM((top + 1 + shared, 2, rows, 2 * count, LANES), jnp.float32),
            pltpu.VMEM((rows * ring, 2 * count, LANES), jnp.float32),
            pltpu.VMEM(tiles.shape, jnp.float32),
            *[pltpu.VMEM(t.shape, t.dtype) for t in tables],
            pltpu.VMEM((count * half, 2 * LANES), jnp.float32),
            pltpu.VMEM((count, LANES), jnp.float32),
            dma((4 + PIECES + len(tables),)),
            dma((PIECES,)),
            dma((PIECES,)),
            dma,
            dma((messages,)),
            dma,
            dma((hops,)),
            dma,
            dma,
        ],
        compiler_params=pltpu.CompilerParams(collective_id=0, has_side_effects=True),
    )(
        traces,
        masks.reshape(rows, ring, 2 * count, channels),
        moveouts.reshape(channels // LANES, LANES),
        tiles,
        *tables,
    )
    return found.transpose(1, 0, 2).reshape(count, lag_count)


def solution(mesh):
    finer = Mesh(mesh.devices.reshape(mesh.shape["grp"], 4, -1, 2), ("grp", "tm_0", "tm_1", "tm_2"))
    axes = ("tm_0", "tm_1", "tm_2")
    return jax.shard_map(
        on_device,
        mesh=finer,
        in_specs=(P("grp", axes), P(axes, None), P("grp"), P(None, "grp")),
        out_specs=P(axes, "grp"),
        check_vma=False,
    )
```

time: 73.6 us -> 63.4 us (0.86)
  Pallas kernels: 71.9 us -> 61 us
    pallas_call x1, Pallas kernels: 71.9 us -> 61 us  [on_device(): pl.pallas_call(functools.partial(matched_kernel, cfg, math.sqrt(channels)...]
where the time goes in v3:
time: 63.4 us; the launch traced here: 62.6 us
  Pallas kernels  61 us (96%)
  local copies, waits for them, and re-layouts  1.57 us (2%)
    pallas_call x1, Pallas kernels, on_device(): pl.pallas_call(functools.partial(matched_kernel, cfg, math.sqrt(channels)...  61 us
    unnamed x1, local copies, waits for them, and re-layouts  1.57 us

profile of v3, /device:TPU:40, one launch (start us, length us, event | category | flops | bytes accessed | tf_op | source)
XLA Modules:
  0.0 62.6 jit_solution(11339147748321861935)
XLA Ops:
  0.0 61.0 %shard_map.100 = f32[64,4,128]{2,1,0:T(4,128)} custom-call(f32[1024,128]{1,0:T(8,128)} %x_hbm.1, s32[4,16,8,1024]{3,2,1,0:T(8,128)} %bitcast.10, s32[8,128]{1,0:T(8,128)} %bitcast.13, f32[256,128]{1,0:T(8,128)} %bitcast.12, bf16[2,144,128]{2,1,0:T(8,128)(2,1)} %constant.12.clone.first_hbm, bf16[2,144,64]{2,1,0:T(8,128)(2,1)} %constant.13.clone.first_half_hbm, ...), custom_call_target="tpu_custom_call" | custom-call | tf_op jit(solution)/shard_map/pallas_call | solution.py:378
  61.0 1.6 %copy.13 = f32[4,8192]{1,0:T(4,128)} copy(f32[4,8192]{1,0:T(4,128)} %bitcast.11) | data formatting | bytes 262144

commit v4 on v3

--- a/solution.py
+++ b/solution.py
@@ -150,12 +150,15 @@
         kept = jnp.where(side == 0, first, second)
         return jnp.where(tops == (side == 0), kept, moved).astype(jnp.float32)
 
-    @pl.loop(0, mask_rows.shape[0])
+    @pl.loop(0, mask_rows.shape[0] // chunk_rows)
     def _(m):
         owner = lax.rem(z + toward * m + ring, ring)
         tiles = [mask_int[a, owner] for a in range(rows)]
         pieces = [pick(tiles[a], tiles[a + 1], side) for side in (core, 1 - core) for a in range(0, rows, 2)]
-        mask_rows[m] = jnp.concatenate(pieces, axis=0).astype(jnp.bfloat16)
+        kept = jnp.concatenate(pieces, axis=0).astype(jnp.bfloat16)
+        at = pl.ds(pl.multiple_of(m * chunk_rows, chunk_rows), chunk_rows)
+        mask_rows[at, :channels] = kept
+        mask_rows[at, channels:] = kept
 
     for p in range(PIECES):
         swaps[p].wait_recv()
@@ -181,17 +184,12 @@
             is_before, is_same, is_after = shift == before, shift == same, shift == after
             for t in range(2):
                 first, second = halves[t, 0, at, :], halves[t, 1, at, :]
-                parts[t, at, :LANES] = jnp.where(is_same, first, jnp.where(is_after, second, zero))
-                parts[t, at, LANES:] = jnp.where(is_before, first, jnp.where(is_same, second, zero))
-
-        full = top - s + 1
-        weights = mask_rows[pl.ds(0, full)].reshape(full * chunk_rows, channels)
-        if shared:
-            weights = jnp.concatenate([weights, mask_rows[full, pl.ds(0, own_rows)]], axis=0)
-        total = mm(weights, parts[0]) + mm(weights, parts[1])
-        partial[s, pl.ds(0, full)] = total[: full * chunk_rows].reshape(full, chunk_rows, 2 * LANES)
-        if shared:
-            partial[s, full, pl.ds(0, own_rows)] = total[full * chunk_rows :]
+                to = pl.ds(pl.multiple_of(t * channels + b * LANES, LANES), LANES)
+                parts[to, :LANES] = jnp.where(is_same, first, jnp.where(is_after, second, zero))
+                parts[to, LANES:] = jnp.where(is_before, first, jnp.where(is_same, second, zero))
+
+        live = pl.ds(0, (top - s + 1) * chunk_rows + shared * own_rows)
+        partial[s, live] = mm(mask_rows[live], parts[...])
 
     contribution(0)
 
@@ -211,18 +209,21 @@
     groups += [(max(high - GROUP + 1, 1), high, chunk_rows) for high in range(top, 0, -GROUP)]
     onward = chip(toward)
 
+    def chunks(m, count, held):
+        return pl.ds(m * chunk_rows, (count - 1) * chunk_rows + held)
+
     def span(s, g):
         low, high, held = groups[g]
         low = max(low, s + 1)
-        return (low - s, high - low + 1, pl.ds(0, held)) if low <= high and s < hops else None
+        return (low - s, high - low + 1, held) if low <= high and s < hops else None
 
     def send_on(s, g):
         found = span(s, g)
         if found is None:
             return
         m, count, held = found
-        src = partial.at[0, pl.ds(m, count), held] if s == 0 else flow.at[s - 1, pl.ds(m, count), held]
-        dst = flow.at[s, pl.ds(m - 1, count), held]
+        src = (partial.at[0] if s == 0 else flow.at[s - 1]).at[chunks(m, count, held)]
+        dst = flow.at[s, chunks(m - 1, count, held)]
         send("flow", src, dst, flow_send, flow_recv.at[slot_of(s, g)], onward)
 
     for g in range(len(groups)):
@@ -269,7 +270,7 @@
     def merge_and_deliver(s):
         wait_for(merge.at[s], merge_recv.at[s])
         own = pl.ds(0, own_rows)
-        deliver(flow[s - 1, 0, own] + partial[s, 0, own] + merge[s], s, 0, 1)
+        deliver(flow[s - 1, own] + partial[s, own] + merge[s], s, 0, 1)
 
     def arrive(s, g):
         arrived = span(s - 1, g)
@@ -277,14 +278,15 @@
             return
         m, count, held = arrived
         m = m - 1
-        wait_for(flow.at[s - 1, pl.ds(m, count), held], flow_recv.at[slot_of(s - 1, g)])
+        wait_for(flow.at[s - 1, chunks(m, count, held)], flow_recv.at[slot_of(s - 1, g)])
         for c in reversed(range(m, m + count)):
+            at = chunks(c, 1, held)
             if s == hops:
-                deliver(flow[s - 1, c, held] + partial[s, c, held], s, c, held.size // own_rows)
+                deliver(flow[s - 1, at] + partial[s, at], s, c, held // own_rows)
             elif c > 0:
-                flow[s - 1, c, held] = flow[s - 1, c, held] + partial[s, c, held]
+                flow[s - 1, at] = flow[s - 1, at] + partial[s, at]
             else:
-                src = flow.at[s - 1, 0, pl.ds(own_rows, own_rows)]
+                src = flow.at[s - 1, pl.ds(own_rows, own_rows)]
                 send("merge", src, merge.at[hops - s], merge_send, merge_recv.at[hops - s], partner)
         send_on(s, g)
 
@@ -302,7 +304,8 @@
 
     for swap in swaps:
         swap.wait_send()
-    wait_for(flow.reshape(-1, chunk_rows, 2 * LANES).at[pl.ds(0, sent["flow"] // math.prod(flow.shape[2:]))], flow_send)
+    flat = flow.reshape(-1, 2 * LANES)
+    wait_for(flat.at[pl.ds(0, sent["flow"] // (2 * LANES))], flow_send)
     wait_for(merge.at[pl.ds(0, sent["merge"] // math.prod(merge.shape[1:]))], merge_send)
     wait_for(landed.at[pl.ds(0, sent["last"] // math.prod(landed.shape[1:]))], last_send)
     for copy in table_copies[3:]:
@@ -377,7 +380,7 @@
     half = tables[2].shape[1]
     found = pl.pallas_call(
         functools.partial(matched_kernel, cfg, math.sqrt(channels)),
-        out_shape=jax.ShapeDtypeStruct((lag_rows, count, LANES), jnp.float32),
+        out_shape=pltpu.VMEM((lag_rows, count, LANES), jnp.float32),
         in_specs=[anywhere] * (4 + len(tables)),
         out_specs=vmem,
         scratch_shapes=[
@@ -385,12 +388,12 @@
             pltpu.VMEM((channels // LANES, LANES), jnp.int32),
             pltpu.VMEM((2, channels, samples), jnp.float32),
             pltpu.VMEM((rows, ring, 2 * count, channels), jnp.int32),
-            pltpu.VMEM((top + 1 + shared, 2 * rows * count, channels), jnp.bfloat16),
+            pltpu.VMEM(((top + 1 + shared) * chunk[0], 2 * channels), jnp.bfloat16),
             pltpu.VMEM((2, 2, channels, samples), jnp.bfloat16),
             pltpu.VMEM((channels, samples), jnp.bfloat16),
-            pltpu.VMEM((2, channels, chip_samples), jnp.bfloat16),
-            pltpu.VMEM((hops + 1, top + 1 + shared, *chunk), jnp.float32),
-            pltpu.VMEM((hops, top + shared, *chunk), jnp.float32),
+            pltpu.VMEM((2 * channels, chip_samples), jnp.bfloat16),
+            pltpu.VMEM((hops + 1, (top + 1 + shared) * chunk[0], chunk[1]), jnp.float32),
+            pltpu.VMEM((hops, (top + shared) * chunk[0], chunk[1]), jnp.float32),
             pltpu.VMEM((hops, rows * count, chip_samples), jnp.float32),
             pltpu.VMEM((top + 1 + shared, 2, rows, 2 * count, LANES), jnp.float32),
             pltpu.VMEM((rows * ring, 2 * count, LANES), jnp.float32),

time: 63.4 us -> 61.8 us (0.975)
  local copies, waits for them, and re-layouts: 1.57 us -> 0.66 us
    unnamed x1, local copies, waits for them, and re-layouts: 1.57 us -> 0.66 us
    pallas_call x1, Pallas kernels: 61 us -> 60.4 us  [on_device(): pl.pallas_call(functools.partial(matched_kernel, cfg, math.sqrt(channels)...]
where the time goes in v4:
time: 61.8 us; the launch traced here: 61 us
  Pallas kernels  60.4 us (98%)
  local copies, waits for them, and re-layouts  0.66 us (1%)
    pallas_call x1, Pallas kernels, on_device(): pl.pallas_call(functools.partial(matched_kernel, cfg, math.sqrt(channels)...  60.4 us

profile of v4, /device:TPU:40, one launch (start us, length us, event | category | flops | bytes accessed | tf_op | source)
XLA Modules:
  0.0 61.0 jit_solution(17664389695813828085)
XLA Ops:
  0.0 60.4 %shard_map.100 = f32[64,4,128]{2,1,0:T(4,128)S(1)} custom-call(f32[1024,128]{1,0:T(8,128)} %x_hbm.1, s32[4,16,8,1024]{3,2,1,0:T(8,128)} %bitcast.11, s32[8,128]{1,0:T(8,128)} %bitcast.13, f32[256,128]{1,0:T(8,128)} %bitcast.12, bf16[2,144,128]{2,1,0:T(8,128)(2,1)} %constant.12.clone.first_hbm, bf16[2,144,64]{2,1,0:T(8,128)(2,1)} %constant.13.clone.first_half_hbm, ...), custom_call_target="tpu_custom_call" | custom-call | tf_op jit(solution)/shard_map/pallas_call | solution.py:381
  60.4 0.7 %copy.13 = f32[4,8192]{1,0:T(4,128)} copy(f32[4,8192]{1,0:T(4,128)S(1)} %bitcast.10) | data formatting | bytes 262144

commit v5 on v4

--- a/solution.py
+++ b/solution.py
@@ -35,7 +35,8 @@
 
 def dot3(left, right):
     (left_hi, left_lo), (right_hi, right_lo) = left, right
-    return mm(left_hi, right_hi) + (mm(left_hi, right_lo) + mm(left_lo, right_hi))
+    lefts = jnp.concatenate([left_hi, left_hi, left_lo], axis=1)
+    return mm(lefts, jnp.concatenate([right_hi, right_lo, right_hi], axis=0))
 
 
 def forward(series, first, twiddle, second):
@@ -110,11 +111,10 @@
 
     lane = lax.broadcasted_iota(jnp.int32, (LANES, LANES), 1)
     mo_copy.wait()
-    swaps = []
     for p in range(PIECES):
         x_copies[p].wait()
 
-        @pl.loop(p * per_piece // LANES, (p + 1) * per_piece // LANES)
+        @pl.loop(p * per_piece // LANES, (p + 1) * per_piece // LANES, unroll=True)
         def _(b):
             at = pl.ds(pl.multiple_of(b * LANES, LANES), LANES)
             spread = jnp.broadcast_to(mo_ref[pl.ds(b, 1), :].astype(jnp.float32), (LANES, LANES))
@@ -128,8 +128,9 @@
             halves[0, core, at, :] = high
             halves[1, core, at, :] = low
 
-        if p == 0:
-            pl.semaphore_wait(barrier, len(peers))
+    pl.semaphore_wait(barrier, len(peers))
+    swaps = []
+    for p in range(PIECES):
         half = pair.at[core, pl.ds(p * per_piece, per_piece)]
         swap = pltpu.make_async_remote_copy(
             src_ref=half, dst_ref=half, send_sem=pair_send.at[p], recv_sem=pair_recv.at[p],
@@ -173,7 +174,7 @@
     zero = jnp.zeros((LANES, LANES), jnp.bfloat16)
     top = hops + outside
 
-    def contribution(s):
+    def select(s):
         twice = jnp.broadcast_to((2 * window_place(s)).astype(jnp.float32), (LANES, LANES))
         before, same, after = ((twice + d).astype(jnp.bfloat16) for d in (-1, 0, 1))
 
@@ -188,10 +189,18 @@
                 parts[to, :LANES] = jnp.where(is_same, first, jnp.where(is_after, second, zero))
                 parts[to, LANES:] = jnp.where(is_before, first, jnp.where(is_same, second, zero))
 
-        live = pl.ds(0, (top - s + 1) * chunk_rows + shared * own_rows)
+    def multiply(s, low=0, high=None):
+        high = (top - s + 1) * chunk_rows + shared * own_rows if high is None else high
+        live = pl.ds(low, high - low)
         partial[s, live] = mm(mask_rows[live], parts[...])
 
-    contribution(0)
+    def contribution(s):
+        select(s)
+        multiply(s)
+
+    select(0)
+    halfway = top // 2 + 1
+    multiply(0, halfway * chunk_rows)
 
     sent = {"flow": 0, "merge": 0, "last": 0}
     slots = {}
@@ -227,7 +236,13 @@
         send("flow", src, dst, flow_send, flow_recv.at[slot_of(s, g)], onward)
 
     for g in range(len(groups)):
+        if groups[g][0] < halfway:
+            continue
         send_on(0, g)
+    multiply(0, chunk_rows, halfway * chunk_rows)
+    for g in range(len(groups)):
+        if groups[g][0] < halfway:
+            send_on(0, g)
 
     def template_spectra():
         templ_copy.wait()

time: 61.8 us -> 60.5 us (0.979)
  Pallas kernels: 60.4 us -> 59.1 us
    pallas_call x1, Pallas kernels: 60.4 us -> 59.1 us  [on_device(): pl.pallas_call(functools.partial(matched_kernel, cfg, math.sqrt(channels)...]
where the time goes in v5:
time: 60.5 us; the launch traced here: 59.8 us
  Pallas kernels  59.1 us (98%)
  local copies, waits for them, and re-layouts  0.66 us (1%)
    pallas_call x1, Pallas kernels, on_device(): pl.pallas_call(functools.partial(matched_kernel, cfg, math.sqrt(channels)...  59.1 us

profile of v5, /device:TPU:40, one launch (start us, length us, event | category | flops | bytes accessed | tf_op | source)
XLA Modules:
  0.0 59.8 jit_solution(8286665520751465930)
XLA Ops:
  0.0 59.1 %shard_map.100 = f32[64,4,128]{2,1,0:T(4,128)S(1)} custom-call(f32[1024,128]{1,0:T(8,128)} %x_hbm.1, s32[4,16,8,1024]{3,2,1,0:T(8,128)} %bitcast.11, s32[8,128]{1,0:T(8,128)} %bitcast.13, f32[256,128]{1,0:T(8,128)} %bitcast.12, bf16[2,144,128]{2,1,0:T(8,128)(2,1)} %constant.12.clone.first_hbm, bf16[2,144,64]{2,1,0:T(8,128)(2,1)} %constant.13.clone.first_half_hbm, ...), custom_call_target="tpu_custom_call" | custom-call | tf_op jit(solution)/shard_map/pallas_call | solution.py:396
  59.1 0.7 %copy.13 = f32[4,8192]{1,0:T(4,128)} copy(f32[4,8192]{1,0:T(4,128)S(1)} %bitcast.10) | data formatting | bytes 262144

commit v6 on v5

--- a/solution.py
+++ b/solution.py
@@ -57,7 +57,7 @@
     out_ref,
     raw, mo_ref, pair, mask_int, mask_rows, halves, shift_at, parts, partial, flow, merge, ready, landed,
     templ_ref, first_ref, first_half_ref, twiddle_ref, second_ref, third_ref, fourth_ref, templ_spec, gain,
-    load_sem, pair_send, pair_recv, flow_send, flow_recv, merge_send, merge_recv, last_send, last_recv,
+    partner_sem, load_sem, pair_send, pair_recv, flow_send, flow_recv, merge_send, merge_recv, last_send, last_recv,
 ):
     rows, ring, hops, outside, shared = cfg
     channels = x_hbm.shape[0]
@@ -92,11 +92,15 @@
     x_copies = [load(x_hbm.at[pl.ds(p * per_piece, per_piece)], raw.at[pl.ds(p * per_piece, per_piece)]) for p in range(PIECES)]
 
     barrier = pltpu.get_barrier_semaphore()
-    peers = [partner, chip(1), chip(-1)]
+    peers = [chip(-toward)]
     for d in range(1, rows):
         peers += [{"tm_0": lax.rem(x + d, rows), "tm_2": c} for c in (core, 1 - core)]
     for where in peers:
         pl.semaphore_signal(barrier, inc=1, device_id=where, device_id_type=MESH)
+
+    @pl.when(core == 1)
+    def _():
+        pl.semaphore_signal(barrier, inc=1, device_id=partner, device_id_type=MESH)
 
     mask_copy = load(masks_hbm, mask_int)
     templ_copy = load(templ_hbm, templ_ref)
@@ -128,7 +132,15 @@
             halves[0, core, at, :] = high
             halves[1, core, at, :] = low
 
-    pl.semaphore_wait(barrier, len(peers))
+    @pl.when(core == 0)
+    def _():
+        pl.semaphore_wait(barrier, len(peers) + 1)
+        pl.semaphore_signal(partner_sem, inc=1, device_id=partner, device_id_type=MESH)
+
+    @pl.when(core == 1)
+    def _():
+        pl.semaphore_wait(partner_sem, 1)
+
     swaps = []
     for p in range(PIECES):
         half = pair.at[core, pl.ds(p * per_piece, per_piece)]
@@ -234,6 +246,10 @@
         src = (partial.at[0] if s == 0 else flow.at[s - 1]).at[chunks(m, count, held)]
         dst = flow.at[s, chunks(m - 1, count, held)]
         send("flow", src, dst, flow_send, flow_recv.at[slot_of(s, g)], onward)
+
+    @pl.when(core == 1)
+    def _():
+        pl.semaphore_wait(barrier, len(peers))
 
     for g in range(len(groups)):
         if groups[g][0] < halfway:
@@ -416,6 +432,7 @@
             *[pltpu.VMEM(t.shape, t.dtype) for t in tables],
             pltpu.VMEM((count * half, 2 * LANES), jnp.float32),
             pltpu.VMEM((count, LANES), jnp.float32),
+            pltpu.SemaphoreType.REGULAR,
             dma((4 + PIECES + len(tables),)),
             dma((PIECES,)),
             dma((PIECES,)),

time: 60.5 us -> 61 us (level)
  no operation moved by 1% of the time
where the time goes in v6:
time: 61 us; the launch traced here: 60.2 us
  Pallas kernels  59.5 us (98%)
  local copies, waits for them, and re-layouts  0.66 us (1%)
    pallas_call x1, Pallas kernels, on_device(): pl.pallas_call(functools.partial(matched_kernel, cfg, math.sqrt(channels)...  59.5 us

profile of v6, /device:TPU:40, one launch (start us, length us, event | category | flops | bytes accessed | tf_op | source)
XLA Modules:
  0.0 60.2 jit_solution(738878965217351663)
XLA Ops:
  0.0 59.5 %shard_map.100 = f32[64,4,128]{2,1,0:T(4,128)S(1)} custom-call(f32[1024,128]{1,0:T(8,128)} %x_hbm.1, s32[4,16,8,1024]{3,2,1,0:T(8,128)} %bitcast.11, s32[8,128]{1,0:T(8,128)} %bitcast.13, f32[256,128]{1,0:T(8,128)} %bitcast.12, bf16[2,144,128]{2,1,0:T(8,128)(2,1)} %constant.12.clone.first_hbm, bf16[2,144,64]{2,1,0:T(8,128)(2,1)} %constant.13.clone.first_half_hbm, ...), custom_call_target="tpu_custom_call" | custom-call | tf_op jit(solution)/shard_map/pallas_call | solution.py:412
  59.5 0.7 %copy.13 = f32[4,8192]{1,0:T(4,128)} copy(f32[4,8192]{1,0:T(4,128)S(1)} %bitcast.10) | data formatting | bytes 262144

commit v7 on v6

--- a/solution.py
+++ b/solution.py
@@ -65,7 +65,9 @@
     x = lax.axis_index("tm_0")
     z = lax.axis_index("tm_1")
     core = lax.axis_index("tm_2")
-    toward = 1 - 2 * core
+    odd = lax.rem(z, 2)
+    way = lax.rem(core + z, 2)
+    toward = 1 - 2 * way
     here = x * ring + z
     partner = {"tm_2": 1 - core}
 
@@ -74,7 +76,7 @@
         return {"tm_0": other // ring, "tm_1": lax.rem(other, ring)}
 
     def window_place(s):
-        return core * hops + toward * s
+        return way * hops + toward * s
 
     def wait_for(ref, sem):
         pltpu.make_async_copy(ref, ref, sem).wait()
@@ -92,13 +94,13 @@
     x_copies = [load(x_hbm.at[pl.ds(p * per_piece, per_piece)], raw.at[pl.ds(p * per_piece, per_piece)]) for p in range(PIECES)]
 
     barrier = pltpu.get_barrier_semaphore()
-    peers = [chip(-toward)]
+    peers = [{**chip(-toward), "tm_2": 1 - core}]
     for d in range(1, rows):
         peers += [{"tm_0": lax.rem(x + d, rows), "tm_2": c} for c in (core, 1 - core)]
     for where in peers:
         pl.semaphore_signal(barrier, inc=1, device_id=where, device_id_type=MESH)
 
-    @pl.when(core == 1)
+    @pl.when(way == 1)
     def _():
         pl.semaphore_signal(barrier, inc=1, device_id=partner, device_id_type=MESH)
 
@@ -132,12 +134,12 @@
             halves[0, core, at, :] = high
             halves[1, core, at, :] = low
 
-    @pl.when(core == 0)
+    @pl.when(way == 0)
     def _():
         pl.semaphore_wait(barrier, len(peers) + 1)
         pl.semaphore_signal(partner_sem, inc=1, device_id=partner, device_id_type=MESH)
 
-    @pl.when(core == 1)
+    @pl.when(way == 1)
     def _():
         pl.semaphore_wait(partner_sem, 1)
 
@@ -167,7 +169,7 @@
     def _(m):
         owner = lax.rem(z + toward * m + ring, ring)
         tiles = [mask_int[a, owner] for a in range(rows)]
-        pieces = [pick(tiles[a], tiles[a + 1], side) for side in (core, 1 - core) for a in range(0, rows, 2)]
+        pieces = [pick(tiles[a], tiles[a + 1], side) for side in (way, 1 - way) for a in range(0, rows, 2)]
         kept = jnp.concatenate(pieces, axis=0).astype(jnp.bfloat16)
         at = pl.ds(pl.multiple_of(m * chunk_rows, chunk_rows), chunk_rows)
         mask_rows[at, :channels] = kept
@@ -228,7 +230,7 @@
 
     groups = [(top + 1, top + 1, own_rows)] if shared else []
     groups += [(max(high - GROUP + 1, 1), high, chunk_rows) for high in range(top, 0, -GROUP)]
-    onward = chip(toward)
+    onward = {**chip(toward), "tm_2": 1 - core}
 
     def chunks(m, count, held):
         return pl.ds(m * chunk_rows, (count - 1) * chunk_rows + held)
@@ -247,7 +249,7 @@
         dst = flow.at[s, chunks(m - 1, count, held)]
         send("flow", src, dst, flow_send, flow_recv.at[slot_of(s, g)], onward)
 
-    @pl.when(core == 1)
+    @pl.when(way == 1)
     def _():
         pl.semaphore_wait(barrier, len(peers))
 
@@ -286,21 +288,24 @@
                 ready[slot, side, a] = jnp.concatenate([piece[:, :LANES], piece[:, LANES:]], axis=0)
         dst = landed.at[lax.rem(here - window_place(s) + blocks, blocks)]
         for side in range(sides):
-            cores = core if side == 0 else 1 - core
             for d in range(rows):
                 if m:
-                    src, where = ready.at[slot, side, d], {"tm_0": d, "tm_1": lax.rem(z + toward * m + ring, ring)}
-                else:
-                    owner = lax.rem(x + d, rows)
-                    src, where = ready.at[slot, side, owner], {"tm_0": owner}
-                if m == 0 and side == 0 and d == 0:
+                    where = {"tm_0": d, "tm_1": lax.rem(z + toward * m + ring, ring), "tm_2": way if side == 0 else 1 - way}
+                    send("last", ready.at[slot, side, d], dst, last_send, last_recv, where)
+                    continue
+                owner = lax.rem(x + d, rows)
+                src = ready.at[slot, 0 if sides == 1 else odd if side == 0 else 1 - odd, owner]
+                if side == 0 and d == 0:
                     pltpu.make_async_copy(src, dst, last_recv).start()
                 else:
-                    send("last", src, dst, last_send, last_recv, {**where, "tm_2": cores})
+                    where = {"tm_0": owner, "tm_2": core if side == 0 else 1 - core}
+                    send("last", src, dst, last_send, last_recv, where)
+
+    own = pl.ds(pl.multiple_of(odd * own_rows, own_rows), own_rows)
+    others = pl.ds(pl.multiple_of((1 - odd) * own_rows, own_rows), own_rows)
 
     def merge_and_deliver(s):
         wait_for(merge.at[s], merge_recv.at[s])
-        own = pl.ds(0, own_rows)
         deliver(flow[s - 1, own] + partial[s, own] + merge[s], s, 0, 1)
 
     def arrive(s, g):
@@ -317,7 +322,7 @@
             elif c > 0:
                 flow[s - 1, at] = flow[s - 1, at] + partial[s, at]
             else:
-                src = flow.at[s - 1, pl.ds(own_rows, own_rows)]
+                src = flow.at[s - 1, others]
                 send("merge", src, merge.at[hops - s], merge_send, merge_recv.at[hops - s], partner)
         send_on(s, g)
 

time: 61 us -> 60.4 us (level)
    pallas_call x1, Pallas kernels: 59.5 us -> 58.9 us  [on_device(): pl.pallas_call(functools.partial(matched_kernel, cfg, math.sqrt(channels)...]
where the time goes in v7:
time: 60.4 us; the launch traced here: 59.6 us
  Pallas kernels  58.9 us (98%)
  local copies, waits for them, and re-layouts  0.66 us (1%)
    pallas_call x1, Pallas kernels, on_device(): pl.pallas_call(functools.partial(matched_kernel, cfg, math.sqrt(channels)...  58.9 us

profile of v7, /device:TPU:40, one launch (start us, length us, event | category | flops | bytes accessed | tf_op | source)
XLA Modules:
  0.0 59.6 jit_solution(16320657736909063836)
XLA Ops:
  0.0 58.9 %shard_map.100 = f32[64,4,128]{2,1,0:T(4,128)S(1)} custom-call(f32[1024,128]{1,0:T(8,128)} %x_hbm.1, s32[4,16,8,1024]{3,2,1,0:T(8,128)} %bitcast.11, s32[8,128]{1,0:T(8,128)} %bitcast.13, f32[256,128]{1,0:T(8,128)} %bitcast.12, bf16[2,144,128]{2,1,0:T(8,128)(2,1)} %constant.12.clone.first_hbm, bf16[2,144,64]{2,1,0:T(8,128)(2,1)} %constant.13.clone.first_half_hbm, ...), custom_call_target="tpu_custom_call" | custom-call | tf_op jit(solution)/shard_map/pallas_call | solution.py:417
  58.9 0.7 %copy.13 = f32[4,8192]{1,0:T(4,128)} copy(f32[4,8192]{1,0:T(4,128)S(1)} %bitcast.10) | data formatting | bytes 262144

commit v8 on v7

--- a/solution.py
+++ b/solution.py
@@ -12,7 +12,7 @@
 
 MESH = pl.DeviceIdType.MESH
 LANES = 128
-GROUP = 1
+HOP = 7.1
 PIECES = 4
 
 
@@ -49,6 +49,28 @@
             jnp.concatenate([re * twiddle[0] - im * twiddle[1], re * twiddle[1] + im * twiddle[0]], axis=1)
         )
     return dot3(split(jnp.concatenate(turned, axis=0)), (second[0], second[1]))
+
+
+def flow_plan(chunks, hops):
+    waiting = [(0.0, 0, g) for g in range(len(chunks))]
+    left = [min(o, hops) for o, _ in chunks]
+    clock, found = 0.0, []
+    while waiting:
+        ready = [task for task in waiting if task[0] <= clock]
+        if not ready:
+            clock = min(waiting)[0]
+            continue
+        task = max(ready, key=lambda task: (left[task[2]] - task[1], -task[2]))
+        waiting.remove(task)
+        _, s, g = task
+        found.append((clock, s, g))
+        clock += chunks[g][1]
+        there = max(clock + HOP, 8.2)
+        if s + 1 < left[g]:
+            waiting.append((there, s + 1, g))
+        else:
+            found.append((there + 1, s + 1, g))
+    return [(s, g) for _, s, g in sorted(found, key=lambda task: task[0])]
 
 
 def matched_kernel(
@@ -228,37 +250,32 @@
         ).start()
         sent[name] += math.prod(src.shape)
 
-    groups = [(top + 1, top + 1, own_rows)] if shared else []
-    groups += [(max(high - GROUP + 1, 1), high, chunk_rows) for high in range(top, 0, -GROUP)]
+    groups = [(top + 1, own_rows)] if shared else []
+    groups += [(o, chunk_rows) for o in range(top, 0, -1)]
     onward = {**chip(toward), "tm_2": 1 - core}
 
-    def chunks(m, count, held):
-        return pl.ds(m * chunk_rows, (count - 1) * chunk_rows + held)
-
-    def span(s, g):
-        low, high, held = groups[g]
-        low = max(low, s + 1)
-        return (low - s, high - low + 1, held) if low <= high and s < hops else None
+    def chunk(m, held):
+        return pl.ds(m * chunk_rows, held)
 
     def send_on(s, g):
-        found = span(s, g)
-        if found is None:
+        o, held = groups[g]
+        if s == min(o, hops):
             return
-        m, count, held = found
-        src = (partial.at[0] if s == 0 else flow.at[s - 1]).at[chunks(m, count, held)]
-        dst = flow.at[s, chunks(m - 1, count, held)]
+        src = (partial.at[0] if s == 0 else flow.at[s - 1]).at[chunk(o - s, held)]
+        dst = flow.at[s, chunk(o - s - 1, held)]
         send("flow", src, dst, flow_send, flow_recv.at[slot_of(s, g)], onward)
 
     @pl.when(way == 1)
     def _():
         pl.semaphore_wait(barrier, len(peers))
 
-    for g in range(len(groups)):
-        if groups[g][0] < halfway:
-            continue
-        send_on(0, g)
+    plan = flow_plan([(o, held / chunk_rows) for o, held in groups], hops)
+    begun = next(k for k, (s, _) in enumerate(plan) if s)
+    for _, g in plan[:begun]:
+        if groups[g][0] >= halfway:
+            send_on(0, g)
     multiply(0, chunk_rows, halfway * chunk_rows)
-    for g in range(len(groups)):
+    for _, g in plan[:begun]:
         if groups[g][0] < halfway:
             send_on(0, g)
 
@@ -274,10 +291,9 @@
             energy = jnp.sqrt(jnp.sum(templates[i] * templates[i], keepdims=True) + 1e-06)
             gain[pl.ds(i, 1), :] = jnp.broadcast_to(1.0 / (scale * energy), (1, LANES))
 
-    contribution(1)
-    contribution(2)
-    template_spectra()
-    todo = list(range(3, hops + 1))
+    todo = list(range(1, hops + 1))
+    for _ in range(min(3, hops)):
+        contribution(todo.pop(0))
 
     def deliver(total, s, m, sides):
         slot = s + m
@@ -309,34 +325,31 @@
         deliver(flow[s - 1, own] + partial[s, own] + merge[s], s, 0, 1)
 
     def arrive(s, g):
-        arrived = span(s - 1, g)
-        if arrived is None:
-            return
-        m, count, held = arrived
-        m = m - 1
-        wait_for(flow.at[s - 1, chunks(m, count, held)], flow_recv.at[slot_of(s - 1, g)])
-        for c in reversed(range(m, m + count)):
-            at = chunks(c, 1, held)
-            if s == hops:
-                deliver(flow[s - 1, at] + partial[s, at], s, c, held // own_rows)
-            elif c > 0:
-                flow[s - 1, at] = flow[s - 1, at] + partial[s, at]
-            else:
-                src = flow.at[s - 1, others]
-                send("merge", src, merge.at[hops - s], merge_send, merge_recv.at[hops - s], partner)
+        o, held = groups[g]
+        m = o - s
+        at = chunk(m, held)
+        wait_for(flow.at[s - 1, at], flow_recv.at[slot_of(s - 1, g)])
+        if s == hops:
+            deliver(flow[s - 1, at] + partial[s, at], s, m, held // own_rows)
+        elif m > 0:
+            flow[s - 1, at] = flow[s - 1, at] + partial[s, at]
+        else:
+            send("merge", flow.at[s - 1, others], merge.at[hops - s], merge_send, merge_recv.at[hops - s], partner)
         send_on(s, g)
 
-    for s in range(1, hops + 1):
-        if s == hops and hops % 2 == 0:
-            merge_and_deliver(hops // 2)
-        for g in range(len(groups)):
-            arrive(s, g)
-            if todo and g in (2, 6):
-                contribution(todo.pop(0))
-        if hops < 2 * s < 2 * hops:
-            merge_and_deliver(s)
-    for s in range((hops - 1) // 2, 0, -1):
+    merges = [hops // 2] + [s for s in range(hops - 1, 0, -1) if s != hops // 2]
+    for s, g in plan[begun:]:
+        if s == 0:
+            send_on(0, g)
+            continue
+        while todo and todo[0] <= s:
+            contribution(todo.pop(0))
+        if s == hops and len(merges) == hops - 1:
+            merge_and_deliver(merges.pop(0))
+        arrive(s, g)
+    for s in merges:
         merge_and_deliver(s)
+    template_spectra()
 
     for swap in swaps:
         swap.wait_send()
@@ -409,7 +422,7 @@
     lag_rows = lag_count // LANES
     tiles = templates.reshape(count, lag_rows, LANES).transpose(1, 0, 2).reshape(lag_rows * count, LANES)
     tables = fourier_tables(length, lag_count)
-    messages = sum(min(high, hops) for high in range(top, 0, -GROUP)) + shared * hops
+    messages = sum(min(high, hops) for high in range(top, 0, -1)) + shared * hops
     vmem = pl.BlockSpec(memory_space=pltpu.VMEM)
     anywhere = pl.BlockSpec(memory_space=pl.ANY)
     dma = pltpu.SemaphoreType.DMA

time: 60.4 us -> 61.1 us (1.012)
  Pallas kernels: 58.9 us -> 60 us
    pallas_call x1, Pallas kernels: 58.9 us -> 60 us  [on_device(): pl.pallas_call(functools.partial(matched_kernel, cfg, math.sqrt(channels)...]
where the time goes in v8:
time: 61.1 us; the launch traced here: 60.7 us
  Pallas kernels  60 us (98%)
  local copies, waits for them, and re-layouts  0.66 us (1%)
    pallas_call x1, Pallas kernels, on_device(): pl.pallas_call(functools.partial(matched_kernel, cfg, math.sqrt(channels)...  60 us

profile of v8, /device:TPU:40, one launch (start us, length us, event | category | flops | bytes accessed | tf_op | source)
XLA Modules:
  0.0 60.7 jit_solution(16293226542171665500)
XLA Ops:
  0.0 60.0 %shard_map.100 = f32[64,4,128]{2,1,0:T(4,128)S(1)} custom-call(f32[1024,128]{1,0:T(8,128)} %x_hbm.1, s32[4,16,8,1024]{3,2,1,0:T(8,128)} %bitcast.11, s32[8,128]{1,0:T(8,128)} %bitcast.13, f32[256,128]{1,0:T(8,128)} %bitcast.12, bf16[2,144,128]{2,1,0:T(8,128)(2,1)} %constant.12.clone.first_hbm, bf16[2,144,64]{2,1,0:T(8,128)(2,1)} %constant.13.clone.first_half_hbm, ...), custom_call_target="tpu_custom_call" | custom-call | tf_op jit(solution)/shard_map/pallas_call | solution.py:430
  60.0 0.7 %copy.13 = f32[4,8192]{1,0:T(4,128)} copy(f32[4,8192]{1,0:T(4,128)S(1)} %bitcast.10) | data formatting | bytes 262144

commit v9 on v7

--- a/solution.py
+++ b/solution.py
@@ -117,7 +117,7 @@
 
     lane = lax.broadcasted_iota(jnp.int32, (LANES, LANES), 1)
     mo_copy.wait()
-    for p in range(PIECES):
+    def roll(p):
         x_copies[p].wait()
 
         @pl.loop(p * per_piece // LANES, (p + 1) * per_piece // LANES, unroll=True)
@@ -134,6 +134,10 @@
             halves[0, core, at, :] = high
             halves[1, core, at, :] = low
 
+    ahead = PIECES // 2
+    for p in range(ahead):
+        roll(p)
+
     @pl.when(way == 0)
     def _():
         pl.semaphore_wait(barrier, len(peers) + 1)
@@ -145,6 +149,8 @@
 
     swaps = []
     for p in range(PIECES):
+        if p >= ahead:
+            roll(p)
         half = pair.at[core, pl.ds(p * per_piece, per_piece)]
         swap = pltpu.make_async_remote_copy(
             src_ref=half, dst_ref=half, send_sem=pair_send.at[p], recv_sem=pair_recv.at[p],
@@ -175,24 +181,14 @@
         mask_rows[at, :channels] = kept
         mask_rows[at, channels:] = kept
 
-    for p in range(PIECES):
-        swaps[p].wait_recv()
-
-        @pl.loop(p * per_piece // LANES, (p + 1) * per_piece // LANES)
-        def _(b):
-            at = pl.ds(pl.multiple_of(b * LANES, LANES), LANES)
-            high, low = split(pair[1 - core, at, :])
-            halves[0, 1 - core, at, :] = high
-            halves[1, 1 - core, at, :] = low
-
     zero = jnp.zeros((LANES, LANES), jnp.bfloat16)
     top = hops + outside
 
-    def select(s):
+    def select(s, start=0, end=channels // LANES):
         twice = jnp.broadcast_to((2 * window_place(s)).astype(jnp.float32), (LANES, LANES))
         before, same, after = ((twice + d).astype(jnp.bfloat16) for d in (-1, 0, 1))
 
-        @pl.loop(0, channels // LANES)
+        @pl.loop(start, end)
         def _(b):
             at = pl.ds(pl.multiple_of(b * LANES, LANES), LANES)
             shift = shift_at[at, :]
@@ -203,6 +199,19 @@
                 parts[to, :LANES] = jnp.where(is_same, first, jnp.where(is_after, second, zero))
                 parts[to, LANES:] = jnp.where(is_before, first, jnp.where(is_same, second, zero))
 
+    for p in range(PIECES):
+        swaps[p].wait_recv()
+        start, end = p * per_piece // LANES, (p + 1) * per_piece // LANES
+
+        @pl.loop(start, end)
+        def _(b):
+            at = pl.ds(pl.multiple_of(b * LANES, LANES), LANES)
+            high, low = split(pair[1 - core, at, :])
+            halves[0, 1 - core, at, :] = high
+            halves[1, 1 - core, at, :] = low
+
+        select(0, start, end)
+
     def multiply(s, low=0, high=None):
         high = (top - s + 1) * chunk_rows + shared * own_rows if high is None else high
         live = pl.ds(low, high - low)
@@ -212,9 +221,8 @@
         select(s)
         multiply(s)
 
-    select(0)
-    halfway = top // 2 + 1
-    multiply(0, halfway * chunk_rows)
+    cuts = [top + 1 + shared, *range(top - 2, 1, -4), 1]
+    multiply(0, cuts[1] * chunk_rows)
 
     sent = {"flow": 0, "merge": 0, "last": 0}
     slots = {}
@@ -253,14 +261,12 @@
     def _():
         pl.semaphore_wait(barrier, len(peers))
 
-    for g in range(len(groups)):
-        if groups[g][0] < halfway:
-            continue
-        send_on(0, g)
-    multiply(0, chunk_rows, halfway * chunk_rows)
-    for g in range(len(groups)):
-        if groups[g][0] < halfway:
-            send_on(0, g)
+    for k, (high, low) in enumerate(zip(cuts, cuts[1:])):
+        if k:
+            multiply(0, low * chunk_rows, high * chunk_rows)
+        for g in range(len(groups)):
+            if low <= groups[g][0] < high:
+                send_on(0, g)
 
     def template_spectra():
         templ_copy.wait()

time: 60.4 us -> 60.3 us (level)
  no operation moved by 1% of the time
where the time goes in v9:
time: 60.3 us; the launch traced here: 59.4 us
  Pallas kernels  58.8 us (98%)
  local copies, waits for them, and re-layouts  0.66 us (1%)
    pallas_call x1, Pallas kernels, on_device(): pl.pallas_call(functools.partial(matched_kernel, cfg, math.sqrt(channels)...  58.8 us

profile of v9, /device:TPU:40, one launch (start us, length us, event | category | flops | bytes accessed | tf_op | source)
XLA Modules:
  0.0 59.4 jit_solution(2493555805731140103)
XLA Ops:
  0.0 58.8 %shard_map.100 = f32[64,4,128]{2,1,0:T(4,128)S(1)} custom-call(f32[1024,128]{1,0:T(8,128)} %x_hbm.1, s32[4,16,8,1024]{3,2,1,0:T(8,128)} %bitcast.11, s32[8,128]{1,0:T(8,128)} %bitcast.13, f32[256,128]{1,0:T(8,128)} %bitcast.12, bf16[2,144,128]{2,1,0:T(8,128)(2,1)} %constant.12.clone.first_hbm, bf16[2,144,64]{2,1,0:T(8,128)(2,1)} %constant.13.clone.first_half_hbm, ...), custom_call_target="tpu_custom_call" | custom-call | tf_op jit(solution)/shard_map/pallas_call | solution.py:423
  58.8 0.7 %copy.13 = f32[4,8192]{1,0:T(4,128)} copy(f32[4,8192]{1,0:T(4,128)S(1)} %bitcast.10) | data formatting | bytes 262144

commit v10 on v9

--- a/solution.py
+++ b/solution.py
@@ -58,6 +58,7 @@
     raw, mo_ref, pair, mask_int, mask_rows, halves, shift_at, parts, partial, flow, merge, ready, landed,
     templ_ref, first_ref, first_half_ref, twiddle_ref, second_ref, third_ref, fourth_ref, templ_spec, gain,
     partner_sem, load_sem, pair_send, pair_recv, flow_send, flow_recv, merge_send, merge_recv, last_send, last_recv,
+    far_send, far_last,
 ):
     rows, ring, hops, outside, shared = cfg
     channels = x_hbm.shape[0]
@@ -213,7 +214,7 @@
         select(0, start, end)
 
     def multiply(s, low=0, high=None):
-        high = (top - s + 1) * chunk_rows + shared * own_rows if high is None else high
+        high = (top - s + 1 + shared) * chunk_rows if high is None else high
         live = pl.ds(low, high - low)
         partial[s, live] = mm(mask_rows[live], parts[...])
 
@@ -224,7 +225,7 @@
     cuts = [top + 1 + shared, *range(top - 2, 1, -4), 1]
     multiply(0, cuts[1] * chunk_rows)
 
-    sent = {"flow": 0, "merge": 0, "last": 0}
+    sent = {"flow": 0, "merge": 0, "last": 0, "far": 0, "far last": 0}
     slots = {}
 
     def slot_of(s, g):
@@ -236,7 +237,7 @@
         ).start()
         sent[name] += math.prod(src.shape)
 
-    groups = [(top + 1, top + 1, own_rows)] if shared else []
+    groups = [(top + 1, top + 1, chunk_rows)] if shared else []
     groups += [(max(high - GROUP + 1, 1), high, chunk_rows) for high in range(top, 0, -GROUP)]
     onward = {**chip(toward), "tm_2": 1 - core}
 
@@ -247,6 +248,9 @@
         low, high, held = groups[g]
         low = max(low, s + 1)
         return (low - s, high - low + 1, held) if low <= high and s < hops else None
+
+    def alone(g):
+        return bool(shared) and g == 0
 
     def send_on(s, g):
         found = span(s, g)
@@ -255,7 +259,16 @@
         m, count, held = found
         src = (partial.at[0] if s == 0 else flow.at[s - 1]).at[chunks(m, count, held)]
         dst = flow.at[s, chunks(m - 1, count, held)]
-        send("flow", src, dst, flow_send, flow_recv.at[slot_of(s, g)], onward)
+        if alone(g):
+            send("far", src, dst, far_send, flow_recv.at[slot_of(s, g)], onward)
+        else:
+            send("flow", src, dst, flow_send, flow_recv.at[slot_of(s, g)], onward)
+
+    def guarded(step, s, g):
+        if alone(g):
+            pl.when(way == 1)(lambda: step(s, g))
+        else:
+            step(s, g)
 
     @pl.when(way == 1)
     def _():
@@ -266,7 +279,7 @@
             multiply(0, low * chunk_rows, high * chunk_rows)
         for g in range(len(groups)):
             if low <= groups[g][0] < high:
-                send_on(0, g)
+                guarded(send_on, 0, g)
 
     def template_spectra():
         templ_copy.wait()
@@ -285,7 +298,7 @@
     template_spectra()
     todo = list(range(3, hops + 1))
 
-    def deliver(total, s, m, sides):
+    def deliver(total, s, m, sides, far=False):
         slot = s + m
         for side in range(sides):
             for a in range(rows):
@@ -297,7 +310,8 @@
             for d in range(rows):
                 if m:
                     where = {"tm_0": d, "tm_1": lax.rem(z + toward * m + ring, ring), "tm_2": way if side == 0 else 1 - way}
-                    send("last", ready.at[slot, side, d], dst, last_send, last_recv, where)
+                    name, sem = ("far last", far_last) if far else ("last", last_send)
+                    send(name, ready.at[slot, side, d], dst, sem, last_recv, where)
                     continue
                 owner = lax.rem(x + d, rows)
                 src = ready.at[slot, 0 if sides == 1 else odd if side == 0 else 1 - odd, owner]
@@ -324,7 +338,7 @@
         for c in reversed(range(m, m + count)):
             at = chunks(c, 1, held)
             if s == hops:
-                deliver(flow[s - 1, at] + partial[s, at], s, c, held // own_rows)
+                deliver(flow[s - 1, at] + partial[s, at], s, c, held // own_rows, alone(g))
             elif c > 0:
                 flow[s - 1, at] = flow[s - 1, at] + partial[s, at]
             else:
@@ -336,7 +350,7 @@
         if s == hops and hops % 2 == 0:
             merge_and_deliver(hops // 2)
         for g in range(len(groups)):
-            arrive(s, g)
+            guarded(arrive, s, g)
             if todo and g in (2, 6):
                 contribution(todo.pop(0))
         if hops < 2 * s < 2 * hops:
@@ -350,6 +364,13 @@
     wait_for(flat.at[pl.ds(0, sent["flow"] // (2 * LANES))], flow_send)
     wait_for(merge.at[pl.ds(0, sent["merge"] // math.prod(merge.shape[1:]))], merge_send)
     wait_for(landed.at[pl.ds(0, sent["last"] // math.prod(landed.shape[1:]))], last_send)
+    if shared:
+
+        @pl.when(way == 1)
+        def _():
+            wait_for(flat.at[pl.ds(0, sent["far"] // (2 * LANES))], far_send)
+            wait_for(landed.at[pl.ds(0, sent["far last"] // math.prod(landed.shape[1:]))], far_last)
+
     for copy in table_copies[3:]:
         copy.wait()
     wait_for(landed, last_recv)
@@ -453,6 +474,8 @@
             dma((hops,)),
             dma,
             dma,
+            dma,
+            dma,
         ],
         compiler_params=pltpu.CompilerParams(collective_id=0, has_side_effects=True),
     )(

time: 60.3 us -> 59.2 us (0.982)
  Pallas kernels: 58.8 us -> 57.8 us
    pallas_call x1, Pallas kernels: 58.8 us -> 57.8 us  [on_device(): pl.pallas_call(functools.partial(matched_kernel, cfg, math.sqrt(channels)...]
where the time goes in v10:
time: 59.2 us; the launch traced here: 58.4 us
  Pallas kernels  57.8 us (98%)
  local copies, waits for them, and re-layouts  0.66 us (1%)
    pallas_call x1, Pallas kernels, on_device(): pl.pallas_call(functools.partial(matched_kernel, cfg, math.sqrt(channels)...  57.8 us

profile of v10, /device:TPU:40, one launch (start us, length us, event | category | flops | bytes accessed | tf_op | source)
XLA Modules:
  0.0 58.4 jit_solution(12938685410465438008)
XLA Ops:
  0.0 57.8 %shard_map.100 = f32[64,4,128]{2,1,0:T(4,128)S(1)} custom-call(f32[1024,128]{1,0:T(8,128)} %x_hbm.1, s32[4,16,8,1024]{3,2,1,0:T(8,128)} %bitcast.11, s32[8,128]{1,0:T(8,128)} %bitcast.13, f32[256,128]{1,0:T(8,128)} %bitcast.12, bf16[2,144,128]{2,1,0:T(8,128)(2,1)} %constant.12.clone.first_hbm, bf16[2,144,64]{2,1,0:T(8,128)(2,1)} %constant.13.clone.first_half_hbm, ...), custom_call_target="tpu_custom_call" | custom-call | tf_op jit(solution)/shard_map/pallas_call | solution.py:444
  57.8 0.7 %copy.13 = f32[4,8192]{1,0:T(4,128)} copy(f32[4,8192]{1,0:T(4,128)S(1)} %bitcast.10) | data formatting | bytes 262144

commit v11 on v10

--- a/solution.py
+++ b/solution.py
@@ -295,7 +295,6 @@
 
     contribution(1)
     contribution(2)
-    template_spectra()
     todo = list(range(3, hops + 1))
 
     def deliver(total, s, m, sides, far=False):
@@ -357,6 +356,8 @@
             merge_and_deliver(s)
     for s in range((hops - 1) // 2, 0, -1):
         merge_and_deliver(s)
+
+    template_spectra()
 
     for swap in swaps:
         swap.wait_send()

time: 59.2 us -> 58.6 us (0.990)
  Pallas kernels: 57.8 us -> 57.1 us
    pallas_call x1, Pallas kernels: 57.8 us -> 57.1 us  [on_device(): pl.pallas_call(functools.partial(matched_kernel, cfg, math.sqrt(channels)...]
where the time goes in v11:
time: 58.6 us; the launch traced here: 57.8 us
  Pallas kernels  57.1 us (97%)
  local copies, waits for them, and re-layouts  0.66 us (1%)
    pallas_call x1, Pallas kernels, on_device(): pl.pallas_call(functools.partial(matched_kernel, cfg, math.sqrt(channels)...  57.1 us

profile of v11, /device:TPU:40, one launch (start us, length us, event | category | flops | bytes accessed | tf_op | source)
XLA Modules:
  0.0 57.8 jit_solution(6501634561505831545)
XLA Ops:
  0.0 57.1 %shard_map.100 = f32[64,4,128]{2,1,0:T(4,128)S(1)} custom-call(f32[1024,128]{1,0:T(8,128)} %x_hbm.1, s32[4,16,8,1024]{3,2,1,0:T(8,128)} %bitcast.11, s32[8,128]{1,0:T(8,128)} %bitcast.13, f32[256,128]{1,0:T(8,128)} %bitcast.12, bf16[2,144,128]{2,1,0:T(8,128)(2,1)} %constant.12.clone.first_hbm, bf16[2,144,64]{2,1,0:T(8,128)(2,1)} %constant.13.clone.first_half_hbm, ...), custom_call_target="tpu_custom_call" | custom-call | tf_op jit(solution)/shard_map/pallas_call | solution.py:445
  57.1 0.7 %copy.13 = f32[4,8192]{1,0:T(4,128)} copy(f32[4,8192]{1,0:T(4,128)S(1)} %bitcast.10) | data formatting | bytes 262144
